TPU v7x, 32 devices: a whole 2x2x4 slice. The times are simulated.
32 devices in a mesh: dom: 16 (over z, y, x), sub: 2 (over core).
Axes of the slice: x: 2, y: 2, z: 4, core: 2. Of those that a mesh axis runs over, the one named last changes fastest.
Arguments:
- rhs: float32 [8192], P(('dom', 'sub')), may hold values from -6 to 6
- diagonal: float32 [8192], P(('dom', 'sub')), may hold values from 1 to 2
- self_raw: float32 [8192, 256], P(('dom', 'sub')), may hold values from -0.046875 to 0.046875
- coupling: float32 [8192, 256], P(('dom', 'sub')), may hold values from -0.046875 to 0.046875
- pattern: int32 [64, 2], P(('dom', 'sub')), may hold values 0 or 1
- prolong: float32 [8192, 128], P(('dom', 'sub')), may hold values from -0.5 to 0.5
- coarse_raw: float32 [4096, 256], P('dom'), may hold values from -0.0234375 to 0.0234375
- coarse_diagonal: float32 [4096], P('dom'), may hold values from 1 to 2
Outputs:
- solution: float32 [8192], P(('dom', 'sub'))
- residual: float32 [8192], P(('dom', 'sub'))
- norms: float32 [3], replicated
All inputs are finite; a program needn't handle non-finite values. No bound on the sum of `pattern` on one device may be relied on, other than what follows from the above.
Results may differ from a plain program's by a relative error of at most 0.0003.
Values sent between devices are 32-bit elements; how exact they have to be, the bound alone decides.
No kernel may reach another device: no remote copies, remote signals or barrier semaphores. Data moves between devices by JAX's collectives and lax.ppermute only.
A program may use at most 64 MiB of HBM per device.

v0:
```python
import jax
import jax.numpy as jnp
from jax import lax
from jax.sharding import PartitionSpec as P

ITERS = 3


OMEGA = 0.7
HIGH = lax.Precision.HIGHEST


def passed_along(value, axis, steps):
    count = lax.axis_size(axis)
    initial, last = (max(0, -steps), min(count, count - steps))
    return lax.ppermute(value, axis, [(source, source + steps) for source in range(initial, last)])


def three_sums(resid, uvec, wvec):
    return lax.psum(
        (jnp.sum(resid * uvec), jnp.sum(wvec * uvec), jnp.sum(resid * resid)), ("dom", "sub")
    )


def per_device(rhs, diagonal, self_raw, coupling, pattern, prolong, coarse_raw, coarse_diagonal):
    width = rhs.shape[0]
    blocks = pattern.shape[0]
    block_rows = width // blocks
    coarse = prolong.shape[1]
    eye = jnp.eye(width, dtype=jnp.float32)
    selfm = 0.5 * (self_raw + self_raw.T) * (1.0 - eye) + eye * diagonal[:, None]
    mask = pattern.reshape(blocks, 1, blocks, 1).astype(jnp.float32)
    mask = jnp.broadcast_to(mask, (blocks, block_rows, blocks, block_rows)).reshape(width, width)
    coup = coupling * mask
    dinv = 1.0 / diagonal
    ceye = jnp.eye(2 * coarse, dtype=jnp.float32)
    cmat = 0.5 * (coarse_raw + coarse_raw.T) * (1.0 - ceye) + ceye * coarse_diagonal[:, None]
    cdinv = 1.0 / coarse_diagonal
    offset = lax.axis_index("sub") * coarse

    def apply(vec):
        upper = passed_along(vec, ("dom", "sub"), -1)
        lower = passed_along(jnp.dot(vec, coup, precision=HIGH), ("dom", "sub"), 1)
        return jnp.dot(selfm, vec, precision=HIGH) + jnp.dot(coup, upper, precision=HIGH) + lower

    def precond(wvec):
        first = OMEGA * dinv * wvec
        resid = wvec - apply(first)
        rcoarse = jnp.dot(resid, prolong, precision=HIGH)
        own_inv = lax.dynamic_slice_in_dim(cdinv, offset, coarse, 0)
        own_rows = lax.dynamic_slice_in_dim(cmat, offset, coarse, 0)
        eone = own_inv * rcoarse
        eboth = lax.all_gather(eone, "sub", axis=0, tiled=True)
        mine = eone + own_inv * (rcoarse - jnp.dot(own_rows, eboth, precision=HIGH))
        second = first + jnp.dot(prolong, mine, precision=HIGH)
        return second + OMEGA * dinv * (wvec - apply(second))

    resid = rhs
    solution = jnp.zeros_like(rhs)
    uvec = precond(resid)
    wvec = apply(uvec)
    zeros = jnp.zeros_like(rhs)
    pvec, svec, qvec, zvec = (zeros, zeros, zeros, zeros)
    gamma_prev = jnp.float32(1.0)
    alpha_prev = jnp.float32(1.0)
    norm_list = []
    for step in range(ITERS):
        mvec = precond(wvec)
        nvec = apply(mvec)
        gamma, delta, rnorm = three_sums(resid, uvec, wvec)
        norm_list.append(rnorm)
        if step == 0:
            beta = jnp.float32(0.0)
            alpha = gamma / delta
        else:
            beta = gamma / gamma_prev
            alpha = gamma / (delta - beta * gamma / alpha_prev)
        zvec = nvec + beta * zvec
        qvec = mvec + beta * qvec
        svec = wvec + beta * svec
        pvec = uvec + beta * pvec
        solution = solution + alpha * pvec
        resid = resid - alpha * svec
        uvec = uvec - alpha * qvec
        wvec = wvec - alpha * zvec
        gamma_prev = gamma
        alpha_prev = alpha
    return (solution, resid, jnp.stack(norm_list))


def solution(mesh):
    in_specs = (
        P(("dom", "sub")),
        P(("dom", "sub")),
        P(("dom", "sub"), None),
        P(("dom", "sub"), None),
        P(("dom", "sub"), None),
        P(("dom", "sub"), None),
        P("dom", None),
        P("dom"),
    )
    out_specs = (P(("dom", "sub")), P(("dom", "sub")), P())
    return jax.shard_map(
        per_device, mesh=mesh, in_specs=in_specs, out_specs=out_specs, check_vma=False
    )
```

profile of v0, /device:TPU:0, one launch (start us, length us, event | category | flops | bytes accessed | tf_op | source)
XLA Modules:
  0.0 227.7 jit_solution(16379148000464561736)
XLA Ops:
  1.4 1.3 collective-permute-start
  3.8 3.1 %collective-permute-start.1 = (f32[256]{0:T(256)S(1)}, f32[256]{0:T(256)S(1)}, u32[]{:S(2)}, u32[]{:S(2)}) collective-permute-start(f32[256]{0:T(256)S(1)} %bitcast.255), channel_id=1, source_target_pairs={{0,1},{1,2},{2,3},{3,4},{4,5},{5,6},{6,7},{7,8},{8,9},{9,10},{10,1... | collective-permute-start | bytes 3080 | tf_op jit(solution)/shard_map/ppermute | solution.py:16
  10.9 4.0 %all-gather = f32[2,1,128]{2,1,0:T(1,128)S(1)} all-gather(f32[1,1,128]{2,1,0:T(1,128)S(1)} %bitcast.253), channel_id=1, replica_groups=mesh['dom'=16,'sub'=2] {'sub'}, dimensions={0}, use_global_device_ids=true | all-gather | bytes 1536 | tf_op jit(solution)/shard_map/all_gather | solution.py:53
  15.4 1.3 collective-permute-start.2
  17.2 3.1 %collective-permute-start.3 = (f32[256]{0:T(256)S(1)}, f32[256]{0:T(256)S(1)}, u32[]{:S(2)}, u32[]{:S(2)}) collective-permute-start(f32[256]{0:T(256)S(1)} %bitcast.263), channel_id=1, source_target_pairs={{0,1},{1,2},{2,3},{3,4},{4,5},{5,6},{6,7},{7,8},{8,9},{9,10},{10,1... | collective-permute-start | bytes 3080 | tf_op jit(solution)/shard_map/ppermute | solution.py:16
  21.1 1.3 collective-permute-start.4
  22.9 4.5 %collective-permute-start.5 = (f32[256]{0:T(256)S(1)}, f32[256]{0:T(256)S(1)}, u32[]{:S(2)}, u32[]{:S(2)}) collective-permute-start(f32[256]{0:T(256)S(1)} %bitcast.265), channel_id=1, source_target_pairs={{0,1},{1,2},{2,3},{3,4},{4,5},{5,6},{6,7},{7,8},{8,9},{9,10},{10,1... | collective-permute-start | bytes 3080 | tf_op jit(solution)/shard_map/ppermute | solution.py:16
  28.2 1.3 collective-permute-start.6
  30.0 4.8 %collective-permute-start.7 = (f32[256]{0:T(256)S(1)}, f32[256]{0:T(256)S(1)}, u32[]{:S(2)}, u32[]{:S(2)}) collective-permute-start(f32[256]{0:T(256)S(1)} %bitcast.267), channel_id=1, source_target_pairs={{0,1},{1,2},{2,3},{3,4},{4,5},{5,6},{6,7},{7,8},{8,9},{9,10},{10,1... | collective-permute-start | bytes 3080 | tf_op jit(solution)/shard_map/ppermute | solution.py:16
  35.7 3.6 %all-gather.1 = f32[2,1,128]{2,1,0:T(1,128)S(1)} all-gather(f32[1,1,128]{2,1,0:T(1,128)S(1)} %bitcast.252), channel_id=1, replica_groups=mesh['dom'=16,'sub'=2] {'sub'}, dimensions={0}, use_global_device_ids=true | all-gather | bytes 1536 | tf_op jit(solution)/shard_map/all_gather | solution.py:53
  39.8 1.3 collective-permute-start.8
  41.6 3.1 %collective-permute-start.9 = (f32[256]{0:T(256)S(1)}, f32[256]{0:T(256)S(1)}, u32[]{:S(2)}, u32[]{:S(2)}) collective-permute-start(f32[256]{0:T(256)S(1)} %bitcast.269), channel_id=1, source_target_pairs={{0,1},{1,2},{2,3},{3,4},{4,5},{5,6},{6,7},{7,8},{8,9},{9,10},{10,1... | collective-permute-start | bytes 3080 | tf_op jit(solution)/shard_map/ppermute | solution.py:16
  46.1 1.3 collective-permute-start.10
  47.9 6.8 %collective-permute-start.11 = (f32[256]{0:T(256)S(1)}, f32[256]{0:T(256)S(1)}, u32[]{:S(2)}, u32[]{:S(2)}) collective-permute-start(f32[256]{0:T(256)S(1)} %bitcast.259), channel_id=1, source_target_pairs={{0,1},{1,2},{2,3},{3,4},{4,5},{5,6},{6,7},{7,8},{8,9},{9,10},{10,1... | collective-permute-start | bytes 3080 | tf_op jit(solution)/shard_map/ppermute | solution.py:16
  54.7 49.2 %all-reduce.2 = (f32[]{:T(128)}, f32[]{:T(128)}) all-reduce(f32[]{:T(128)} %get-tuple-element.7, f32[]{:T(128)} %get-tuple-element.8), channel_id=1, replica_groups=mesh['dom'=16,'sub'=2] {'dom','sub'}, use_global_device_ids=true, to_apply=%region_1.0 | all-reduce | flops 2 | bytes 16 | tf_op jit(solution)/shard_map/psum | solution.py:20
  106.2 1.3 collective-permute-start.12
  108.0 41.2 %all-reduce.1 = (f32[]{:T(128)}, f32[]{:T(128)}) all-reduce(f32[]{:T(128)} %get-tuple-element.4, f32[]{:T(128)} %get-tuple-element.3), channel_id=1, replica_groups=mesh['dom'=16,'sub'=2] {'dom','sub'}, use_global_device_ids=true, to_apply=%region_5.0 | all-reduce | flops 2 | bytes 16 | tf_op jit(solution)/shard_map/psum | solution.py:20
  150.6 1.3 collective-permute-start.13
  155.6 4.5 %all-gather.2 = f32[2,1,128]{2,1,0:T(1,128)S(1)} all-gather(f32[1,1,128]{2,1,0:T(1,128)S(1)} %bitcast.251), channel_id=1, replica_groups=mesh['dom'=16,'sub'=2] {'sub'}, dimensions={0}, use_global_device_ids=true | all-gather | bytes 1536 | tf_op jit(solution)/shard_map/all_gather | solution.py:53
  160.5 1.3 collective-permute-start.14
  162.3 3.1 %collective-permute-start.15 = (f32[256]{0:T(256)S(1)}, f32[256]{0:T(256)S(1)}, u32[]{:S(2)}, u32[]{:S(2)}) collective-permute-start(f32[256]{0:T(256)S(1)} %bitcast.271), channel_id=1, source_target_pairs={{0,1},{1,2},{2,3},{3,4},{4,5},{5,6},{6,7},{7,8},{8,9},{9,10},{10,1... | collective-permute-start | bytes 3080 | tf_op jit(solution)/shard_map/ppermute | solution.py:16
  168.0 4.1 %collective-permute-start.17 = (f32[256]{0:T(256)S(1)}, f32[256]{0:T(256)S(1)}, u32[]{:S(2)}, u32[]{:S(2)}) collective-permute-start(f32[256]{0:T(256)S(1)} %bitcast.261), channel_id=1, source_target_pairs={{0,1},{1,2},{2,3},{3,4},{4,5},{5,6},{6,7},{7,8},{8,9},{9,10},{10,1... | collective-permute-start | bytes 3080 | tf_op jit(solution)/shard_map/ppermute | solution.py:16
  173.5 47.3 %all-reduce = (f32[]{:T(128)}, f32[]{:T(128)}, f32[1]{0:T(128)}, f32[1]{0:T(128)}, f32[1]{0:T(128)}) all-reduce(f32[]{:T(128)} %get-tuple-element.10, f32[]{:T(128)} %get-tuple-element.11, f32[1]{0:T(128)} %bitcast.82, f32[1]{0:T(128)} %bitcast.81, f32[1]{0:T(128)} %bitcast.80), channel_id=1, replica_groups=mesh['dom'=16,'sub'=2] {'dom','sub'}, use_global_device_ids=true, to_apply=%region_9.0 | all-reduce | flops 5 | bytes 40 | tf_op jit(solution)/shard_map/psum | solution.py:20
  224.7 2.4 %pad_maximum_fusion = f32[3]{0:T(128)} fusion(f32[1]{0:T(128)} %get-tuple-element.14, f32[1]{0:T(128)} %get-tuple-element.15, f32[1]{0:T(128)} %get-tuple-element.16), kind=kLoop, calls=%fused_computation.59 | loop fusion | flops 6 | bytes 24 | tf_op jit(solution)/shard_map/stack | solution.py:88
  (96 shorter events, 20.6 us)
Async XLA Ops:
  0.6 10.1 %copy-start = (f32[256,128]{1,0:T(8,128)S(1)}, f32[256,128]{1,0:T(8,128)}, u32[]{:S(2)}) copy-start(f32[256,128]{1,0:T(8,128)} %param.13) | copy-start | bytes 393220
  0.6 2.9 %copy-start.3 = (f32[256,256]{1,0:T(8,128)S(1)}, f32[256,256]{1,0:T(8,128)}, u32[]{:S(2)}) copy-start(f32[256,256]{1,0:T(8,128)} %param.11) | copy-start | bytes 786436
  1.4 8.3 %collective-permute-start = (f32[256]{0:T(256)S(1)}, f32[256]{0:T(256)S(1)}, u32[]{:S(2)}, u32[]{:S(2)}) collective-permute-start(f32[256]{0:T(256)S(1)} %get-tuple-element.30), channel_id=1, source_target_pairs={{1,0},{2,1},{3,2},{4,3},{5,4},{6,5},{7,6},{8,7},{9,8},{10,9},{11,1... | collective-permute-start | bytes 3080 | tf_op jit(solution)/shard_map/ppermute | solution.py:16
  3.6 3.3 %copy-start.1 = (f32[256,256]{1,0:T(8,128)S(1)}, f32[256,256]{1,0:T(8,128)}, u32[]{:S(2)}) copy-start(f32[256,256]{1,0:T(8,128)} %param.10) | copy-start | bytes 786436
  3.8 6.2 %collective-permute-start.1 = (f32[256]{0:T(256)S(1)}, f32[256]{0:T(256)S(1)}, u32[]{:S(2)}, u32[]{:S(2)}) collective-permute-start(f32[256]{0:T(256)S(1)} %bitcast.255), channel_id=1, source_target_pairs={{0,1},{1,2},{2,3},{3,4},{4,5},{5,6},{6,7},{7,8},{8,9},{9,10},{10,1... | collective-permute-start | bytes 3080 | tf_op jit(solution)/shard_map/ppermute | solution.py:16
  6.9 0.7 copy-start.5
  7.7 1.0 copy-start.2
  9.9 0.7 copy-start.4
  15.4 4.9 %collective-permute-start.2 = (f32[256]{0:T(256)S(1)}, f32[256]{0:T(256)S(1)}, u32[]{:S(2)}, u32[]{:S(2)}) collective-permute-start(f32[256]{0:T(256)S(1)} %add.151), channel_id=1, source_target_pairs={{1,0},{2,1},{3,2},{4,3},{5,4},{6,5},{7,6},{8,7},{9,8},{10,9},{11,1... | collective-permute-start | bytes 3080 | tf_op jit(solution)/shard_map/ppermute | solution.py:16
  17.2 3.9 %collective-permute-start.3 = (f32[256]{0:T(256)S(1)}, f32[256]{0:T(256)S(1)}, u32[]{:S(2)}, u32[]{:S(2)}) collective-permute-start(f32[256]{0:T(256)S(1)} %bitcast.263), channel_id=1, source_target_pairs={{0,1},{1,2},{2,3},{3,4},{4,5},{5,6},{6,7},{7,8},{8,9},{9,10},{10,1... | collective-permute-start | bytes 3080 | tf_op jit(solution)/shard_map/ppermute | solution.py:16
  21.1 6.3 %collective-permute-start.4 = (f32[256]{0:T(256)S(1)}, f32[256]{0:T(256)S(1)}, u32[]{:S(2)}, u32[]{:S(2)}) collective-permute-start(f32[256]{0:T(256)S(1)} %multiply_add_fusion.4), channel_id=1, source_target_pairs={{1,0},{2,1},{3,2},{4,3},{5,4},{6,5},{7,6},{8,7},{9,8},{10,9},{11,1... | collective-permute-start | bytes 3080 | tf_op jit(solution)/shard_map/ppermute | solution.py:16
  22.9 5.3 %collective-permute-start.5 = (f32[256]{0:T(256)S(1)}, f32[256]{0:T(256)S(1)}, u32[]{:S(2)}, u32[]{:S(2)}) collective-permute-start(f32[256]{0:T(256)S(1)} %bitcast.265), channel_id=1, source_target_pairs={{0,1},{1,2},{2,3},{3,4},{4,5},{5,6},{6,7},{7,8},{8,9},{9,10},{10,1... | collective-permute-start | bytes 3080 | tf_op jit(solution)/shard_map/ppermute | solution.py:16
  28.2 6.6 %collective-permute-start.6 = (f32[256]{0:T(256)S(1)}, f32[256]{0:T(256)S(1)}, u32[]{:S(2)}, u32[]{:S(2)}) collective-permute-start(f32[256]{0:T(256)S(1)} %get-tuple-element.26), channel_id=1, source_target_pairs={{1,0},{2,1},{3,2},{4,3},{5,4},{6,5},{7,6},{8,7},{9,8},{10,9},{11,1... | collective-permute-start | bytes 3080 | tf_op jit(solution)/shard_map/ppermute | solution.py:16
  30.0 5.6 %collective-permute-start.7 = (f32[256]{0:T(256)S(1)}, f32[256]{0:T(256)S(1)}, u32[]{:S(2)}, u32[]{:S(2)}) collective-permute-start(f32[256]{0:T(256)S(1)} %bitcast.267), channel_id=1, source_target_pairs={{0,1},{1,2},{2,3},{3,4},{4,5},{5,6},{6,7},{7,8},{8,9},{9,10},{10,1... | collective-permute-start | bytes 3080 | tf_op jit(solution)/shard_map/ppermute | solution.py:16
  39.8 4.9 %collective-permute-start.8 = (f32[256]{0:T(256)S(1)}, f32[256]{0:T(256)S(1)}, u32[]{:S(2)}, u32[]{:S(2)}) collective-permute-start(f32[256]{0:T(256)S(1)} %add.160), channel_id=1, source_target_pairs={{1,0},{2,1},{3,2},{4,3},{5,4},{6,5},{7,6},{8,7},{9,8},{10,9},{11,1... | collective-permute-start | bytes 3080 | tf_op jit(solution)/shard_map/ppermute | solution.py:16
  41.6 3.9 %collective-permute-start.9 = (f32[256]{0:T(256)S(1)}, f32[256]{0:T(256)S(1)}, u32[]{:S(2)}, u32[]{:S(2)}) collective-permute-start(f32[256]{0:T(256)S(1)} %bitcast.269), channel_id=1, source_target_pairs={{0,1},{1,2},{2,3},{3,4},{4,5},{5,6},{6,7},{7,8},{8,9},{9,10},{10,1... | collective-permute-start | bytes 3080 | tf_op jit(solution)/shard_map/ppermute | solution.py:16
  46.1 59.1 %collective-permute-start.10 = (f32[256]{0:T(256)S(1)}, f32[256]{0:T(256)S(1)}, u32[]{:S(2)}, u32[]{:S(2)}) collective-permute-start(f32[256]{0:T(256)S(1)} %get-tuple-element.32), channel_id=1, source_target_pairs={{1,0},{2,1},{3,2},{4,3},{5,4},{6,5},{7,6},{8,7},{9,8},{10,9},{11,1... | collective-permute-start | bytes 3080 | tf_op jit(solution)/shard_map/ppermute | solution.py:16
  47.9 57.6 %collective-permute-start.11 = (f32[256]{0:T(256)S(1)}, f32[256]{0:T(256)S(1)}, u32[]{:S(2)}, u32[]{:S(2)}) collective-permute-start(f32[256]{0:T(256)S(1)} %bitcast.259), channel_id=1, source_target_pairs={{0,1},{1,2},{2,3},{3,4},{4,5},{5,6},{6,7},{7,8},{8,9},{9,10},{10,1... | collective-permute-start | bytes 3080 | tf_op jit(solution)/shard_map/ppermute | solution.py:16
  106.2 48.8 %collective-permute-start.12 = (f32[256]{0:T(256)S(1)}, f32[256]{0:T(256)S(1)}, u32[]{:S(2)}, u32[]{:S(2)}) collective-permute-start(f32[256]{0:T(256)S(1)} %mul.220), channel_id=1, source_target_pairs={{1,0},{2,1},{3,2},{4,3},{5,4},{6,5},{7,6},{8,7},{9,8},{10,9},{11,1... | collective-permute-start | bytes 3080 | tf_op jit(solution)/shard_map/ppermute | solution.py:16
  150.6 4.7 %collective-permute-start.13 = (f32[256]{0:T(256)S(1)}, f32[256]{0:T(256)S(1)}, u32[]{:S(2)}, u32[]{:S(2)}) collective-permute-start(f32[256]{0:T(256)S(1)} %bitcast.257), channel_id=1, source_target_pairs={{0,1},{1,2},{2,3},{3,4},{4,5},{5,6},{6,7},{7,8},{8,9},{9,10},{10,1... | collective-permute-start | bytes 3080 | tf_op jit(solution)/shard_map/ppermute | solution.py:16
  160.5 4.9 %collective-permute-start.14 = (f32[256]{0:T(256)S(1)}, f32[256]{0:T(256)S(1)}, u32[]{:S(2)}, u32[]{:S(2)}) collective-permute-start(f32[256]{0:T(256)S(1)} %add.172), channel_id=1, source_target_pairs={{1,0},{2,1},{3,2},{4,3},{5,4},{6,5},{7,6},{8,7},{9,8},{10,9},{11,1... | collective-permute-start | bytes 3080 | tf_op jit(solution)/shard_map/ppermute | solution.py:16
  162.3 3.9 %collective-permute-start.15 = (f32[256]{0:T(256)S(1)}, f32[256]{0:T(256)S(1)}, u32[]{:S(2)}, u32[]{:S(2)}) collective-permute-start(f32[256]{0:T(256)S(1)} %bitcast.271), channel_id=1, source_target_pairs={{0,1},{1,2},{2,3},{3,4},{4,5},{5,6},{6,7},{7,8},{8,9},{9,10},{10,1... | collective-permute-start | bytes 3080 | tf_op jit(solution)/shard_map/ppermute | solution.py:16
  166.2 5.9 %collective-permute-start.16 = (f32[256]{0:T(256)S(1)}, f32[256]{0:T(256)S(1)}, u32[]{:S(2)}, u32[]{:S(2)}) collective-permute-start(f32[256]{0:T(256)S(1)} %multiply_add_fusion.1), channel_id=1, source_target_pairs={{1,0},{2,1},{3,2},{4,3},{5,4},{6,5},{7,6},{8,7},{9,8},{10,9},{11,1... | collective-permute-start | bytes 3080 | tf_op jit(solution)/shard_map/ppermute | solution.py:16
  168.0 4.9 %collective-permute-start.17 = (f32[256]{0:T(256)S(1)}, f32[256]{0:T(256)S(1)}, u32[]{:S(2)}, u32[]{:S(2)}) collective-permute-start(f32[256]{0:T(256)S(1)} %bitcast.261), channel_id=1, source_target_pairs={{0,1},{1,2},{2,3},{3,4},{4,5},{5,6},{6,7},{7,8},{8,9},{9,10},{10,1... | collective-permute-start | bytes 3080 | tf_op jit(solution)/shard_map/ppermute | solution.py:16
  (1 other events, 0.7 us)
where the time goes:
time: 229 us; the launch traced here: 228 us
  blocking collectives  150 us (66%)
  starting transfers between devices  45.3 us (20%)
  between operations  10.8 us (5%)
  matrix products  8.57 us (4%)
  other arithmetic  6.91 us (3%)
  waiting for transfers between devices  3.15 us (1%)
  local copies, waits for them, and re-layouts  3.1 us (1%)
    psum x3, blocking collectives, three_sums(): lax.psum((jnp.sum(resid * uvec), jnp.sum(wvec * uvec), jnp.sum(resid * re...  138 us
    ppermute x18, starting transfers between devices, passed_along(): lax.ppermute(value, axis, [(source, source + steps) for source in range(i...  45.3 us
    all_gather x3, blocking collectives, precond(): eboth = lax.all_gather(eone, 'sub', axis=0, tiled=True)  12.2 us
  transfers between devices with their start and end apart: 18, of which 6 were waited for; matrix products, arithmetic and copies ran while one was open for 4% of the time, Pallas kernels for 0%

commit v1 on v0

--- a/solution.py
+++ b/solution.py
@@ -17,9 +17,13 @@
 
 
 def three_sums(resid, uvec, wvec):
-    return lax.psum(
-        (jnp.sum(resid * uvec), jnp.sum(wvec * uvec), jnp.sum(resid * resid)), ("dom", "sub")
-    )
+    axes = ("dom", "sub")
+    count = lax.axis_size(axes)
+    parts = jnp.stack([jnp.sum(resid * uvec), jnp.sum(wvec * uvec), jnp.sum(resid * resid)])
+    sent = jnp.broadcast_to(jnp.pad(parts, (0, 125))[None], (count, 128))
+    got = lax.all_to_all(sent, axes, 0, 0, tiled=True)
+    sums = jnp.sum(got, axis=0)
+    return sums[0], sums[1], sums[2]
 
 
 def per_device(rhs, diagonal, self_raw, coupling, pattern, prolong, coarse_raw, coarse_diagonal):

time: 229 us -> 139 us (0.61)
  blocking collectives: 150 us -> 28 us
  starting transfers between devices: 45.3 us -> 63.2 us
  other arithmetic: 6.91 us -> 12.7 us
  waiting for transfers between devices: 3.15 us -> 7.89 us
  local copies, waits for them, and re-layouts: 3.1 us -> 6.2 us
    psum x3 -> x0, blocking collectives: 138 us -> none  [three_sums(): lax.psum((jnp.sum(resid * uvec), jnp.sum(wvec * uvec), jnp.sum(resid * re...]
    all_to_all x0 -> x2, starting transfers between devices: none -> 21 us  [three_sums(): got = lax.all_to_all(sent, axes, 0, 0, tiled=True)]
    all_to_all x0 -> x1, blocking collectives: none -> 17.3 us  [three_sums(): got = lax.all_to_all(sent, axes, 0, 0, tiled=True)]
    another operation x0 -> x3, other arithmetic: none -> 5.82 us  [three_sums(): jnp.stack([jnp.sum(resid * uvec), jnp.sum(wvec * uvec), jnp.sum(resid * r...]
    all_to_all x0 -> x2, waiting for transfers between devices: none -> 4.74 us  [three_sums(): got = lax.all_to_all(sent, axes, 0, 0, tiled=True)]
    ppermute x18, starting transfers between devices: 45.3 us -> 42.2 us  [passed_along(): lax.ppermute(value, axis, [(source, source + steps) for source in range(i...]
  transfers between devices with their start and end apart: 18 -> 20, of which waited for: 6 -> 7; matrix products, arithmetic and copies ran while one was open for 4% -> 10% of each run, Pallas kernels for 0% -> 0%
where the time goes in v1:
time: 139 us; the launch traced here: 138 us
  starting transfers between devices  63.2 us (45%)
  blocking collectives  28 us (20%)
  other arithmetic  12.7 us (9%)
  between operations  10.9 us (8%)
  matrix products  8.57 us (6%)
  waiting for transfers between devices  7.89 us (6%)
  local copies, waits for them, and re-layouts  6.2 us (4%)
    ppermute x18, starting transfers between devices, passed_along(): lax.ppermute(value, axis, [(source, source + steps) for source in range(i...  42.2 us
    all_to_all x2, starting transfers between devices, three_sums(): got = lax.all_to_all(sent, axes, 0, 0, tiled=True)  21 us
    all_to_all x1, blocking collectives, three_sums(): got = lax.all_to_all(sent, axes, 0, 0, tiled=True)  17.3 us
    all_gather x3, blocking collectives, precond(): eboth = lax.all_gather(eone, 'sub', axis=0, tiled=True)  10.7 us
    another operation x3, other arithmetic, three_sums(): jnp.stack([jnp.sum(resid * uvec), jnp.sum(wvec * uvec), jnp.sum(resid * r...  5.82 us
    all_to_all x2, waiting for transfers between devices, three_sums(): got = lax.all_to_all(sent, axes, 0, 0, tiled=True)  4.74 us
    ppermute x18, waiting for transfers between devices, passed_along(): lax.ppermute(value, axis, [(source, source + steps) for source in range(i...  3.15 us
    unnamed x16, local copies, waits for them, and re-layouts  2.89 us
  transfers between devices with their start and end apart: 20, of which 7 were waited for; matrix products, arithmetic and copies ran while one was open for 10% of the time, Pallas kernels for 0%

profile of v1, /device:TPU:0, one launch (start us, length us, event | category | flops | bytes accessed | tf_op | source)
XLA Modules:
  0.0 137.5 jit_solution(15279249522349811511)
XLA Ops:
  3.8 3.1 %collective-permute-start.1 = (f32[256]{0:T(256)S(1)}, f32[256]{0:T(256)S(1)}, u32[]{:S(2)}, u32[]{:S(2)}) collective-permute-start(f32[256]{0:T(256)S(1)} %bitcast.273), channel_id=1, source_target_pairs={{0,1},{1,2},{2,3},{3,4},{4,5},{5,6},{6,7},{7,8},{8,9},{9,10},{10,1... | collective-permute-start | bytes 3080 | tf_op jit(solution)/shard_map/ppermute | solution.py:16
  10.9 4.0 %all-gather = f32[2,1,128]{2,1,0:T(1,128)S(1)} all-gather(f32[1,1,128]{2,1,0:T(1,128)S(1)} %bitcast.271), channel_id=1, replica_groups=mesh['dom'=16,'sub'=2] {'sub'}, dimensions={0}, use_global_device_ids=true | all-gather | bytes 1536 | tf_op jit(solution)/shard_map/all_gather | solution.py:57
  15.4 1.3 collective-permute-start.2
  17.2 3.1 %collective-permute-start.3 = (f32[256]{0:T(256)S(1)}, f32[256]{0:T(256)S(1)}, u32[]{:S(2)}, u32[]{:S(2)}) collective-permute-start(f32[256]{0:T(256)S(1)} %bitcast.281), channel_id=1, source_target_pairs={{0,1},{1,2},{2,3},{3,4},{4,5},{5,6},{6,7},{7,8},{8,9},{9,10},{10,1... | collective-permute-start | bytes 3080 | tf_op jit(solution)/shard_map/ppermute | solution.py:16
  22.9 4.5 %collective-permute-start.5 = (f32[256]{0:T(256)S(1)}, f32[256]{0:T(256)S(1)}, u32[]{:S(2)}, u32[]{:S(2)}) collective-permute-start(f32[256]{0:T(256)S(1)} %bitcast.283), channel_id=1, source_target_pairs={{0,1},{1,2},{2,3},{3,4},{4,5},{5,6},{6,7},{7,8},{8,9},{9,10},{10,1... | collective-permute-start | bytes 3080 | tf_op jit(solution)/shard_map/ppermute | solution.py:16
  30.0 4.8 %collective-permute-start.7 = (f32[256]{0:T(256)S(1)}, f32[256]{0:T(256)S(1)}, u32[]{:S(2)}, u32[]{:S(2)}) collective-permute-start(f32[256]{0:T(256)S(1)} %bitcast.285), channel_id=1, source_target_pairs={{0,1},{1,2},{2,3},{3,4},{4,5},{5,6},{6,7},{7,8},{8,9},{9,10},{10,1... | collective-permute-start | bytes 3080 | tf_op jit(solution)/shard_map/ppermute | solution.py:16
  35.7 3.6 %all-gather.1 = f32[2,1,128]{2,1,0:T(1,128)S(1)} all-gather(f32[1,1,128]{2,1,0:T(1,128)S(1)} %bitcast.270), channel_id=1, replica_groups=mesh['dom'=16,'sub'=2] {'sub'}, dimensions={0}, use_global_device_ids=true | all-gather | bytes 1536 | tf_op jit(solution)/shard_map/all_gather | solution.py:57
  39.8 1.3 collective-permute-start.8
  41.6 3.1 %collective-permute-start.9 = (f32[256]{0:T(256)S(1)}, f32[256]{0:T(256)S(1)}, u32[]{:S(2)}, u32[]{:S(2)}) collective-permute-start(f32[256]{0:T(256)S(1)} %bitcast.287), channel_id=1, source_target_pairs={{0,1},{1,2},{2,3},{3,4},{4,5},{5,6},{6,7},{7,8},{8,9},{9,10},{10,1... | collective-permute-start | bytes 3080 | tf_op jit(solution)/shard_map/ppermute | solution.py:16
  46.6 1.3 collective-permute-start.10
  48.0 2.0 %select_maximum_fusion.4 = f32[128]{0:T(128)S(1)} fusion(f32[1]{0:T(128)} %bitcast.30, f32[1]{0:T(128)} %bitcast.29, f32[1]{0:T(128)} %bitcast.22), kind=kLoop, calls=%fused_computation.63 | loop fusion | flops 768 | bytes 524 | tf_op jit(solution)/shard_map/stack | solution.py:22
  50.6 17.7 %all-to-all-start = ((f32[32,1,128]{2,1,0:T(1,128)}), f32[32,1,128]{2,1,0:T(1,128)S(1)}, u32[]{:S(2)}, u32[]{:S(2)}) async-start(f32[32,1,128]{2,1,0:T(1,128)} %broadcast_in_dim.9), calls=%async_computation | async-start | bytes 32768 | tf_op jit(solution)/shard_map/all_to_all | solution.py:24
  68.3 2.2 %collective-permute-start.11 = (f32[256]{0:T(256)S(1)}, f32[256]{0:T(256)S(1)}, u32[]{:S(2)}, u32[]{:S(2)}) collective-permute-start(f32[256]{0:T(256)S(1)} %bitcast.274), channel_id=1, source_target_pairs={{0,1},{1,2},{2,3},{3,4},{4,5},{5,6},{6,7},{7,8},{8,9},{9,10},{10,1... | collective-permute-start | bytes 3080 | tf_op jit(solution)/shard_map/ppermute | solution.py:16
  70.8 4.7 %all-to-all-done = f32[32,1,128]{2,1,0:T(1,128)S(1)} async-done(((f32[32,1,128]{2,1,0:T(1,128)}), f32[32,1,128]{2,1,0:T(1,128)S(1)}, u32[]{:S(2)}, u32[]{:S(2)}) %all-to-all-start) | async-done | bytes 16416 | tf_op jit(solution)/shard_map/all_to_all | solution.py:24
  78.7 1.3 collective-permute-start.12
  80.0 1.9 %select_maximum_fusion.2 = f32[128]{0:T(128)S(1)} fusion(f32[1]{0:T(128)} %bitcast.62, f32[1]{0:T(128)} %bitcast.61, f32[1]{0:T(128)} %bitcast.54), kind=kLoop, calls=%fused_computation.61 | loop fusion | flops 768 | bytes 524 | tf_op jit(solution)/shard_map/stack | solution.py:22
  82.5 3.3 %all-to-all-start.1 = ((f32[32,1,128]{2,1,0:T(1,128)}), f32[32,1,128]{2,1,0:T(1,128)S(1)}, u32[]{:S(2)}, u32[]{:S(2)}) async-start(f32[32,1,128]{2,1,0:T(1,128)} %broadcast_in_dim.10), calls=%async_computation.1 | async-start | bytes 32768 | tf_op jit(solution)/shard_map/all_to_all | solution.py:24
  85.8 2.2 %collective-permute-start.13 = (f32[256]{0:T(256)S(1)}, f32[256]{0:T(256)S(1)}, u32[]{:S(2)}, u32[]{:S(2)}) collective-permute-start(f32[256]{0:T(256)S(1)} %bitcast.276), channel_id=1, source_target_pairs={{0,1},{1,2},{2,3},{3,4},{4,5},{5,6},{6,7},{7,8},{8,9},{9,10},{10,1... | collective-permute-start | bytes 3080 | tf_op jit(solution)/shard_map/ppermute | solution.py:16
  88.9 3.0 %all-gather.2 = f32[2,1,128]{2,1,0:T(1,128)S(1)} all-gather(f32[1,1,128]{2,1,0:T(1,128)S(1)} %bitcast.269), channel_id=1, replica_groups=mesh['dom'=16,'sub'=2] {'sub'}, dimensions={0}, use_global_device_ids=true | all-gather | bytes 1536 | tf_op jit(solution)/shard_map/all_gather | solution.py:57
  94.2 3.1 %collective-permute-start.15 = (f32[256]{0:T(256)S(1)}, f32[256]{0:T(256)S(1)}, u32[]{:S(2)}, u32[]{:S(2)}) collective-permute-start(f32[256]{0:T(256)S(1)} %bitcast.289), channel_id=1, source_target_pairs={{0,1},{1,2},{2,3},{3,4},{4,5},{5,6},{6,7},{7,8},{8,9},{9,10},{10,1... | collective-permute-start | bytes 3080 | tf_op jit(solution)/shard_map/ppermute | solution.py:16
  99.9 4.6 %collective-permute-start.17 = (f32[256]{0:T(256)S(1)}, f32[256]{0:T(256)S(1)}, u32[]{:S(2)}, u32[]{:S(2)}) collective-permute-start(f32[256]{0:T(256)S(1)} %bitcast.275), channel_id=1, source_target_pairs={{0,1},{1,2},{2,3},{3,4},{4,5},{5,6},{6,7},{7,8},{8,9},{9,10},{10,1... | collective-permute-start | bytes 3080 | tf_op jit(solution)/shard_map/ppermute | solution.py:16
  110.8 1.9 %select_maximum_fusion = f32[128]{0:T(128)S(1)} fusion(f32[1]{0:T(128)} %bitcast.94, f32[1]{0:T(128)} %bitcast.93, f32[1]{0:T(128)} %bitcast.86), kind=kLoop, calls=%fused_computation.59 | loop fusion | flops 768 | bytes 524 | tf_op jit(solution)/shard_map/stack | solution.py:22
  112.8 17.3 %all_to_all.18 = f32[32,1,128]{2,1,0:T(1,128)S(1)} all-to-all(f32[32,1,128]{2,1,0:T(1,128)S(1)} %broadcast_in_dim.11), channel_id=1, replica_groups=mesh['dom'=16,'sub'=2] {'dom','sub'}, dimensions={0} | all-to-all | bytes 32768 | tf_op jit(solution)/shard_map/all_to_all | solution.py:24
  134.5 2.4 %pad_maximum_fusion = f32[3]{0:T(128)} fusion(f32[1]{0:T(128)} %get-tuple-element.30, f32[1]{0:T(128)} %get-tuple-element.27, f32[1]{0:T(128)} %get-tuple-element.24), kind=kLoop, calls=%fused_computation.66 | loop fusion | flops 6 | bytes 24 | tf_op jit(solution)/shard_map/stack | solution.py:92
  (110 shorter events, 28.8 us)
Async XLA Ops:
  0.6 10.1 %copy-start = (f32[256,128]{1,0:T(8,128)S(1)}, f32[256,128]{1,0:T(8,128)}, u32[]{:S(2)}) copy-start(f32[256,128]{1,0:T(8,128)} %param.13) | copy-start | bytes 393220
  0.6 2.9 %copy-start.3 = (f32[256,256]{1,0:T(8,128)S(1)}, f32[256,256]{1,0:T(8,128)}, u32[]{:S(2)}) copy-start(f32[256,256]{1,0:T(8,128)} %param.11) | copy-start | bytes 786436
  1.4 8.3 %collective-permute-start = (f32[256]{0:T(256)S(1)}, f32[256]{0:T(256)S(1)}, u32[]{:S(2)}, u32[]{:S(2)}) collective-permute-start(f32[256]{0:T(256)S(1)} %get-tuple-element.21), channel_id=1, source_target_pairs={{1,0},{2,1},{3,2},{4,3},{5,4},{6,5},{7,6},{8,7},{9,8},{10,9},{11,1... | collective-permute-start | bytes 3080 | tf_op jit(solution)/shard_map/ppermute | solution.py:16
  3.6 3.3 %copy-start.1 = (f32[256,256]{1,0:T(8,128)S(1)}, f32[256,256]{1,0:T(8,128)}, u32[]{:S(2)}) copy-start(f32[256,256]{1,0:T(8,128)} %param.10) | copy-start | bytes 786436
  3.8 6.2 %collective-permute-start.1 = (f32[256]{0:T(256)S(1)}, f32[256]{0:T(256)S(1)}, u32[]{:S(2)}, u32[]{:S(2)}) collective-permute-start(f32[256]{0:T(256)S(1)} %bitcast.273), channel_id=1, source_target_pairs={{0,1},{1,2},{2,3},{3,4},{4,5},{5,6},{6,7},{7,8},{8,9},{9,10},{10,1... | collective-permute-start | bytes 3080 | tf_op jit(solution)/shard_map/ppermute | solution.py:16
  7.7 1.0 copy-start.2
  15.4 4.9 %collective-permute-start.2 = (f32[256]{0:T(256)S(1)}, f32[256]{0:T(256)S(1)}, u32[]{:S(2)}, u32[]{:S(2)}) collective-permute-start(f32[256]{0:T(256)S(1)} %add.139), channel_id=1, source_target_pairs={{1,0},{2,1},{3,2},{4,3},{5,4},{6,5},{7,6},{8,7},{9,8},{10,9},{11,1... | collective-permute-start | bytes 3080 | tf_op jit(solution)/shard_map/ppermute | solution.py:16
  17.2 3.9 %collective-permute-start.3 = (f32[256]{0:T(256)S(1)}, f32[256]{0:T(256)S(1)}, u32[]{:S(2)}, u32[]{:S(2)}) collective-permute-start(f32[256]{0:T(256)S(1)} %bitcast.281), channel_id=1, source_target_pairs={{0,1},{1,2},{2,3},{3,4},{4,5},{5,6},{6,7},{7,8},{8,9},{9,10},{10,1... | collective-permute-start | bytes 3080 | tf_op jit(solution)/shard_map/ppermute | solution.py:16
  21.1 6.3 %collective-permute-start.4 = (f32[256]{0:T(256)S(1)}, f32[256]{0:T(256)S(1)}, u32[]{:S(2)}, u32[]{:S(2)}) collective-permute-start(f32[256]{0:T(256)S(1)} %multiply_add_fusion.4), channel_id=1, source_target_pairs={{1,0},{2,1},{3,2},{4,3},{5,4},{6,5},{7,6},{8,7},{9,8},{10,9},{11,1... | collective-permute-start | bytes 3080 | tf_op jit(solution)/shard_map/ppermute | solution.py:16
  22.9 5.3 %collective-permute-start.5 = (f32[256]{0:T(256)S(1)}, f32[256]{0:T(256)S(1)}, u32[]{:S(2)}, u32[]{:S(2)}) collective-permute-start(f32[256]{0:T(256)S(1)} %bitcast.283), channel_id=1, source_target_pairs={{0,1},{1,2},{2,3},{3,4},{4,5},{5,6},{6,7},{7,8},{8,9},{9,10},{10,1... | collective-permute-start | bytes 3080 | tf_op jit(solution)/shard_map/ppermute | solution.py:16
  28.2 6.6 %collective-permute-start.6 = (f32[256]{0:T(256)S(1)}, f32[256]{0:T(256)S(1)}, u32[]{:S(2)}, u32[]{:S(2)}) collective-permute-start(f32[256]{0:T(256)S(1)} %get-tuple-element.17), channel_id=1, source_target_pairs={{1,0},{2,1},{3,2},{4,3},{5,4},{6,5},{7,6},{8,7},{9,8},{10,9},{11,1... | collective-permute-start | bytes 3080 | tf_op jit(solution)/shard_map/ppermute | solution.py:16
  30.0 5.6 %collective-permute-start.7 = (f32[256]{0:T(256)S(1)}, f32[256]{0:T(256)S(1)}, u32[]{:S(2)}, u32[]{:S(2)}) collective-permute-start(f32[256]{0:T(256)S(1)} %bitcast.285), channel_id=1, source_target_pairs={{0,1},{1,2},{2,3},{3,4},{4,5},{5,6},{6,7},{7,8},{8,9},{9,10},{10,1... | collective-permute-start | bytes 3080 | tf_op jit(solution)/shard_map/ppermute | solution.py:16
  39.8 4.9 %collective-permute-start.8 = (f32[256]{0:T(256)S(1)}, f32[256]{0:T(256)S(1)}, u32[]{:S(2)}, u32[]{:S(2)}) collective-permute-start(f32[256]{0:T(256)S(1)} %add.148), channel_id=1, source_target_pairs={{1,0},{2,1},{3,2},{4,3},{5,4},{6,5},{7,6},{8,7},{9,8},{10,9},{11,1... | collective-permute-start | bytes 3080 | tf_op jit(solution)/shard_map/ppermute | solution.py:16
  41.6 3.9 %collective-permute-start.9 = (f32[256]{0:T(256)S(1)}, f32[256]{0:T(256)S(1)}, u32[]{:S(2)}, u32[]{:S(2)}) collective-permute-start(f32[256]{0:T(256)S(1)} %bitcast.287), channel_id=1, source_target_pairs={{0,1},{1,2},{2,3},{3,4},{4,5},{5,6},{6,7},{7,8},{8,9},{9,10},{10,1... | collective-permute-start | bytes 3080 | tf_op jit(solution)/shard_map/ppermute | solution.py:16
  46.6 23.9 %collective-permute-start.10 = (f32[256]{0:T(256)S(1)}, f32[256]{0:T(256)S(1)}, u32[]{:S(2)}, u32[]{:S(2)}) collective-permute-start(f32[256]{0:T(256)S(1)} %get-tuple-element.23), channel_id=1, source_target_pairs={{1,0},{2,1},{3,2},{4,3},{5,4},{6,5},{7,6},{8,7},{9,8},{10,9},{11,1... | collective-permute-start | bytes 3080 | tf_op jit(solution)/shard_map/ppermute | solution.py:16
  50.6 24.9 %all-to-all-start = ((f32[32,1,128]{2,1,0:T(1,128)}), f32[32,1,128]{2,1,0:T(1,128)S(1)}, u32[]{:S(2)}, u32[]{:S(2)}) async-start(f32[32,1,128]{2,1,0:T(1,128)} %broadcast_in_dim.9), calls=%async_computation | async-start | bytes 32768 | tf_op jit(solution)/shard_map/all_to_all | solution.py:24
  68.3 9.1 %collective-permute-start.11 = (f32[256]{0:T(256)S(1)}, f32[256]{0:T(256)S(1)}, u32[]{:S(2)}, u32[]{:S(2)}) collective-permute-start(f32[256]{0:T(256)S(1)} %bitcast.274), channel_id=1, source_target_pairs={{0,1},{1,2},{2,3},{3,4},{4,5},{5,6},{6,7},{7,8},{8,9},{9,10},{10,1... | collective-permute-start | bytes 3080 | tf_op jit(solution)/shard_map/ppermute | solution.py:16
  78.7 9.3 %collective-permute-start.12 = (f32[256]{0:T(256)S(1)}, f32[256]{0:T(256)S(1)}, u32[]{:S(2)}, u32[]{:S(2)}) collective-permute-start(f32[256]{0:T(256)S(1)} %mul.222), channel_id=1, source_target_pairs={{1,0},{2,1},{3,2},{4,3},{5,4},{6,5},{7,6},{8,7},{9,8},{10,9},{11,1... | collective-permute-start | bytes 3080 | tf_op jit(solution)/shard_map/ppermute | solution.py:16
  82.5 22.3 %all-to-all-start.1 = ((f32[32,1,128]{2,1,0:T(1,128)}), f32[32,1,128]{2,1,0:T(1,128)S(1)}, u32[]{:S(2)}, u32[]{:S(2)}) async-start(f32[32,1,128]{2,1,0:T(1,128)} %broadcast_in_dim.10), calls=%async_computation.1 | async-start | bytes 32768 | tf_op jit(solution)/shard_map/all_to_all | solution.py:24
  85.8 3.0 %collective-permute-start.13 = (f32[256]{0:T(256)S(1)}, f32[256]{0:T(256)S(1)}, u32[]{:S(2)}, u32[]{:S(2)}) collective-permute-start(f32[256]{0:T(256)S(1)} %bitcast.276), channel_id=1, source_target_pairs={{0,1},{1,2},{2,3},{3,4},{4,5},{5,6},{6,7},{7,8},{8,9},{9,10},{10,1... | collective-permute-start | bytes 3080 | tf_op jit(solution)/shard_map/ppermute | solution.py:16
  92.4 4.9 %collective-permute-start.14 = (f32[256]{0:T(256)S(1)}, f32[256]{0:T(256)S(1)}, u32[]{:S(2)}, u32[]{:S(2)}) collective-permute-start(f32[256]{0:T(256)S(1)} %add.160), channel_id=1, source_target_pairs={{1,0},{2,1},{3,2},{4,3},{5,4},{6,5},{7,6},{8,7},{9,8},{10,9},{11,1... | collective-permute-start | bytes 3080 | tf_op jit(solution)/shard_map/ppermute | solution.py:16
  94.2 3.9 %collective-permute-start.15 = (f32[256]{0:T(256)S(1)}, f32[256]{0:T(256)S(1)}, u32[]{:S(2)}, u32[]{:S(2)}) collective-permute-start(f32[256]{0:T(256)S(1)} %bitcast.289), channel_id=1, source_target_pairs={{0,1},{1,2},{2,3},{3,4},{4,5},{5,6},{6,7},{7,8},{8,9},{9,10},{10,1... | collective-permute-start | bytes 3080 | tf_op jit(solution)/shard_map/ppermute | solution.py:16
  98.1 6.4 %collective-permute-start.16 = (f32[256]{0:T(256)S(1)}, f32[256]{0:T(256)S(1)}, u32[]{:S(2)}, u32[]{:S(2)}) collective-permute-start(f32[256]{0:T(256)S(1)} %multiply_add_fusion.1), channel_id=1, source_target_pairs={{1,0},{2,1},{3,2},{4,3},{5,4},{6,5},{7,6},{8,7},{9,8},{10,9},{11,1... | collective-permute-start | bytes 3080 | tf_op jit(solution)/shard_map/ppermute | solution.py:16
  99.9 10.3 %collective-permute-start.17 = (f32[256]{0:T(256)S(1)}, f32[256]{0:T(256)S(1)}, u32[]{:S(2)}, u32[]{:S(2)}) collective-permute-start(f32[256]{0:T(256)S(1)} %bitcast.275), channel_id=1, source_target_pairs={{0,1},{1,2},{2,3},{3,4},{4,5},{5,6},{6,7},{7,8},{8,9},{9,10},{10,1... | collective-permute-start | bytes 3080 | tf_op jit(solution)/shard_map/ppermute | solution.py:16
  (3 other events, 2.1 us)

commit v2 on v0

v2 whole, which is shorter than its diff:
```python
import functools

import jax
import jax.numpy as jnp
from jax import lax
from jax.experimental import pallas as pl
from jax.experimental.pallas import tpu as pltpu
from jax.sharding import PartitionSpec as P

AXES = ("dom", "sub")
OMEGA = 0.7
LANES = 128
GROUP = 16
F32 = jnp.float32


def local_call(body, outs, *args, smem=(), scratch=(), flops=200_000):
    spaces = [pltpu.SMEM if i in smem else pltpu.VMEM for i in range(len(args))]
    return pl.pallas_call(
        body,
        out_shape=[jax.ShapeDtypeStruct(s, F32) for s in outs],
        in_specs=[pl.BlockSpec(memory_space=s) for s in spaces],
        out_specs=[pl.BlockSpec(memory_space=pltpu.VMEM) for _ in outs],
        scratch_shapes=list(scratch),
        cost_estimate=pl.CostEstimate(flops=flops, bytes_accessed=1000, transcendentals=0),
        compiler_params=pltpu.CompilerParams(vmem_limit_bytes=8 * 1024 * 1024),
    )(*args)


def unit(rows, cols):
    shape = (rows, cols)
    return lax.broadcasted_iota(jnp.int32, shape, 0) == lax.broadcasted_iota(jnp.int32, shape, 1)


def over_lanes(a):
    return jnp.sum(a, axis=1, keepdims=True)


def over_rows(a):
    return jnp.sum(a, axis=0, keepdims=True)


def as_row(col):
    eye = unit(LANES, LANES)
    pieces = [
        over_rows(jnp.where(eye, col[k : k + LANES], 0.0)) for k in range(0, col.shape[0], LANES)
    ]
    return jnp.concatenate(pieces, axis=1)


def as_col(row):
    eye = unit(LANES, LANES)
    pieces = [
        over_lanes(jnp.where(eye, row[:, k : k + LANES], 0.0))
        for k in range(0, row.shape[1], LANES)
    ]
    return jnp.concatenate(pieces, axis=0)


def two_sum(a, b):
    s = a + b
    t = s - a
    return s, (a - (s - t)) + (b - t)


def halves(a):
    t = 4097.0 * a
    hi = t - (t - a)
    return hi, a - hi


def two_prod(a, b):
    p = a * b
    ah, al = halves(a)
    bh, bl = halves(b)
    return p, ((ah * bh - p) + ah * bl + al * bh) + al * bl


def pair_add(a, b):
    s, e = two_sum(a[0], b[0])
    e = e + (a[1] + b[1])
    hi = s + e
    return hi, e - (hi - s)


def pair_mul(a, b):
    p, e = two_prod(a[0], b[0])
    e = e + (a[0] * b[1] + a[1] * b[0])
    hi = p + e
    return hi, e - (hi - p)


def start_body(rhs, diag, coup, pattern, cm, sent):
    blocks = pattern.shape[0]
    step = coup.shape[0] // blocks
    for i in range(blocks):
        for j in range(blocks):
            keep = pattern[i, j].astype(F32)
            rows, cols = pl.ds(i * step, step), pl.ds(j * step, step)
            cm[rows, cols] = coup[rows, cols] * keep
    scale = OMEGA / diag[...]
    first = scale * rhs[...]
    sent[0:1] = over_rows(cm[...] * as_col(first))
    sent[1:2] = first
    sent[2:3] = scale


def setup_body(raw, diag, craw, cdiag, pro, cm, packed, fmat):
    width = raw.shape[0]
    coarse = pro.shape[1]
    eye = unit(width, width)
    r = raw[...]
    packed[0:width] = jnp.where(eye, diag[...] * (1.0 - 1.0 / OMEGA), 0.5 * (r + r.T))
    packed[width : 2 * width] = cm[...]
    packed[2 * width :] = pro[...].T
    q = craw[...]
    inv = 1.0 / cdiag[...]
    full = jnp.where(unit(2 * coarse, 2 * coarse), inv, -0.5 * (q + q.T) * inv * as_col(inv))
    core = lax.axis_index("sub")

    @pl.when(core == 0)
    def _():
        fmat[...] = full

    @pl.when(core != 0)
    def _():
        swapped = jnp.concatenate([full[coarse:], full[:coarse]], axis=0)
        fmat[...] = jnp.concatenate([swapped[:, coarse:], swapped[:, :coarse]], axis=1)


def inner_edge_body(packed, got, ein, eint):
    width = ein.shape[0]
    core = lax.axis_index("sub")

    @pl.when(core == 0)
    def _():
        c = packed[width : 2 * width]
        ein[...] = c
        eint[...] = c.T

    @pl.when(core != 0)
    def _():
        c = got[width : 2 * width]
        ein[...] = c.T
        eint[...] = c


def outer_edge_body(cm, got, eout, eoutt):
    core = lax.axis_index("sub")

    @pl.when(core == 0)
    def _():
        c = got[...]
        eout[...] = c.T
        eoutt[...] = c

    @pl.when(core != 0)
    def _():
        c = cm[...]
        eout[...] = c
        eoutt[...] = c.T


def restrict_first_body(sent, inner, outer, packed, cm, pro, out):
    width = sent.shape[1]
    zero = lax.axis_index("sub") == 0
    raw = jnp.where(zero, inner[1:2], outer[1:2])
    done = jnp.where(zero, outer[0:1], inner[0:1])
    r = over_lanes(
        packed[0:width] * sent[1:2] + cm[...] * raw + jnp.where(unit(width, width), done, 0.0)
    )
    out[...] = -over_rows(pro[...] * r)


def restrict_local_body(state, packed, ein, pro, out):
    width = state.shape[1]
    r = over_lanes(packed[0:width] * state[1:2] + ein[...] * state[2:3])
    out[...] = over_rows(pro[...] * r)


def restrict_body(local, x1o, eout, pro, out):
    r = over_lanes(eout[...] * x1o[...])
    out[...] = -(local[...] + over_rows(pro[...] * r))


def coarse_body(ca, cb, state, fmat, packed, other, ein, scale, out):
    width = state.shape[1]
    coarse = ca.shape[1]
    both = jnp.concatenate([ca[...], cb[...]], axis=1)
    e = over_lanes(fmat[...] * both)
    xa = state[1:2] + over_rows(packed[2 * width :] * e[:coarse])
    xb = state[2:3] + over_rows(other[2 * width :] * e[coarse:])
    v = over_lanes(packed[0:width] * xa + ein[...] * xb)
    out[0:1] = xa
    out[1:2] = scale[0:1] * (state[0:1] - as_row(v))


def edge_local_body(sent, eoutt, scale, out):
    out[...] = scale[2:3] * as_row(over_lanes(eoutt[...] * sent[0:1]))


def edge_body(sent, got, own, eout, scale, out):
    u = as_row(over_lanes(eout[...] * got[0:1]))
    mo = got[1:2] - own[...]
    out[0:1] = sent[1:2] - scale[0:1] * u
    out[1:2] = as_row(over_lanes(eout[...] * mo))


def apply_body(sent, got, packed, other, ein, eint, scale, state, x1):
    width = sent.shape[1]
    ma, mb = sent[0:1], got[0:1]
    va = over_lanes(packed[0:width] * ma + ein[...] * mb)
    vb = over_lanes(other[0:width] * mb + eint[...] * ma)
    na = as_row(va) + sent[1:2] + ma / scale[0:1]
    nb = as_row(vb) + got[1:2] + mb / scale[1:2]
    xa = scale[0:1] * na
    state[0:1] = na
    state[1:2] = xa
    state[2:3] = scale[1:2] * nb
    x1[...] = xa


def scale_body(sent, inner, outer, rhs, scale, state):
    scale[0:1] = sent[2:3]
    scale[1:2] = inner[2:3]
    scale[2:3] = outer[2:3]
    state[0:1] = rhs[...]
    state[1:2] = sent[1:2]
    state[2:3] = inner[1:2]


def gram_body(*refs):
    lefts, rights, out, xs, ys = refs[:4], refs[4:7], refs[7], refs[8], refs[9]
    xs[...] = jnp.zeros_like(xs)
    ys[...] = jnp.zeros_like(ys)
    for i in range(3):
        for j in range(3):
            for group, a, b in (
                (0, lefts[i], rights[j]),
                (1, lefts[i + 1], rights[j]),
                (2, lefts[i], lefts[j]),
            ):
                at = group * GROUP + 3 * i + j
                xs[at : at + 1] = a[0:1]
                ys[at : at + 1] = b[0:1]
    hi, lo = two_prod(xs[...], ys[...])
    parts = [(hi[:, k : k + LANES], lo[:, k : k + LANES]) for k in range(0, hi.shape[1], LANES)]
    total = functools.reduce(pair_add, parts)
    step = LANES // 2
    while step:
        total = pair_add(total, tuple(pltpu.roll(t, step, 1) for t in total))
        step //= 2
    eye = unit(xs.shape[0], LANES)
    hi, lo = (over_rows(jnp.where(eye, t, 0.0)) for t in total)
    row = hi + pltpu.roll(jnp.broadcast_to(lo, (8, LANES)), LANES // 2, 1)[0:1]
    out[...] = jnp.broadcast_to(row, out.shape)


def finish_body(got, b, w0, n0, n1, u0, m0, m1, sol, res, norms):
    full = got[...]
    rows = full.shape[0]
    tiles = [full[k : k + 8] for k in range(0, rows, 8)]
    pairs = [(t, pltpu.roll(t, LANES // 2, 1)) for t in tiles]
    while len(pairs) > 1:
        rest = pairs[len(pairs) // 2 * 2 :]
        pairs = [pair_add(pairs[k], pairs[k + 1]) for k in range(0, len(pairs) - 1, 2)] + rest
    gram = pairs[0]
    for step in (4, 2, 1):
        gram = pair_add(gram, tuple(pltpu.roll(t, step, 0) for t in gram))
    lane = lax.broadcasted_iota(jnp.int32, (8, LANES), 1)
    term = lane % GROUP
    left, right = term // 3, term % 3
    valid = (term < 9) & (lane < 3 * GROUP)
    gram = tuple(jnp.where(valid, t, 0.0) for t in gram)

    def at(value, where):
        return over_lanes(jnp.where(lane == where, value, 0.0))

    def form(c1, c2):
        def coefficient(index):
            hi = jnp.where(index == 0, 1.0, jnp.where(index == 1, -c1[0], c2[0]))
            lo = jnp.where(index == 0, 0.0, jnp.where(index == 1, -c1[1], c2[1]))
            return hi, lo

        total = pair_mul(pair_mul(coefficient(left), coefficient(right)), gram)
        for step in (8, 4, 2, 1):
            total = pair_add(total, tuple(pltpu.roll(t, LANES - step, 1) for t in total))
        return tuple(at(total[0], g * GROUP) for g in range(3))

    gamma0, delta0, rho0 = (at(gram[0], g * GROUP) for g in range(3))
    zero = jnp.zeros_like(gamma0)
    alpha0 = gamma0 / delta0
    gamma1, delta1, rho1 = form((alpha0, zero), (zero, zero))
    beta1 = gamma1 / gamma0
    alpha1 = gamma1 / (delta1 - beta1 * gamma1 / alpha0)
    c1 = pair_add((alpha0, zero), pair_mul((alpha1, zero), two_sum(zero + 1.0, beta1)))
    gamma2, delta2, rho2 = form(c1, two_prod(alpha0, alpha1))
    beta2 = gamma2 / gamma1
    alpha2 = gamma2 / (delta2 - beta2 * gamma2 / alpha1)

    a0, a1, a2, b1, b2 = (t[0:1] for t in (alpha0, alpha1, alpha2, beta1, beta2))
    rb, rw0, rn0, rn1, ru0, rm0, rm1 = (t[0:1] for t in (b, w0, n0, n1, u0, m0, m1))
    r1 = rb - a0 * rw0
    u1 = ru0 - a0 * rm0
    w1 = rw0 - a0 * rn0
    s1 = w1 + b1 * rw0
    p1 = u1 + b1 * ru0
    z1 = (rn0 - a0 * rn1) + b1 * rn0
    q1 = (rm0 - a0 * rm1) + b1 * rm0
    r2 = r1 - a1 * s1
    u2 = u1 - a1 * q1
    w2 = w1 - a1 * z1
    s2 = w2 + b2 * s1
    p2 = u2 + b2 * p1
    sol[...] = a0 * ru0 + a1 * p1 + a2 * p2
    res[...] = r2 - a2 * s2
    where = lane[0:1]
    row = jnp.where(where == 0, rho0[0:1], jnp.where(where == 1, rho1[0:1], rho2[0:1]))
    norms[...] = row[:, :3]


def per_device(rhs, diagonal, self_raw, coupling, pattern, prolong, coarse_raw, coarse_diagonal):
    width, coarse = rhs.shape[0], prolong.shape[1]
    chips = lax.axis_size("dom")
    inner = [(2 * g + c, 2 * g + 1 - c) for g in range(chips) for c in range(2)]
    up = [(2 * g + 1, 2 * g + 2) for g in range(chips - 1)]
    outer = up + [(b, a) for a, b in up]
    square, row = (width, width), (1, width)

    def move(value, pairs):
        return lax.ppermute(value, AXES, pairs)

    rhs_row, diag_row = rhs.reshape(row), diagonal.reshape(row)
    cm, sent = local_call(
        start_body, [square, (3, width)], rhs_row, diag_row, coupling, pattern, smem=(3,)
    )
    from_outer = move(sent, outer)
    from_inner = move(sent, inner)
    packed, fmat = local_call(
        setup_body,
        [(2 * width + coarse, width), (2 * coarse, 2 * coarse)],
        self_raw,
        diag_row,
        coarse_raw,
        coarse_diagonal.reshape(1, 2 * coarse),
        prolong,
        cm,
        flops=1_000_000,
    )
    other = move(packed, inner)
    cm_up = move(cm, up)
    scale, state = local_call(
        scale_body, [(3, width), (3, width)], sent, from_inner, from_outer, rhs_row
    )
    c_own = local_call(
        restrict_first_body, [(1, coarse)], sent, from_inner, from_outer, packed, cm, prolong
    )[0]
    ein, eint = local_call(inner_edge_body, [square, square], packed, other)
    eout, eoutt = local_call(outer_edge_body, [square, square], cm, cm_up)

    lefts, rights = [rhs_row], []
    for cycle in range(3):
        if cycle:
            x1o = move(x1, outer)
            local = local_call(restrict_local_body, [(1, coarse)], state, packed, ein, prolong)[0]
            c_own = local_call(restrict_body, [(1, coarse)], local, x1o, eout, prolong)[0]
        c_other = move(c_own, inner)
        half = local_call(
            coarse_body, [(2, width)], c_own, c_other, state, fmat, packed, other, ein, scale
        )[0]
        got = move(half, outer)
        own = local_call(edge_local_body, [row], half, eoutt, scale)[0]
        mt = local_call(edge_body, [(2, width)], half, got, own, eout, scale)[0]
        mt_other = move(mt, inner)
        state, x1 = local_call(
            apply_body, [(3, width), row], mt, mt_other, packed, other, ein, eint, scale
        )
        lefts.append(state)
        rights.append(mt)

    count = 2 * chips
    parts = local_call(
        gram_body,
        [(count, LANES)],
        *lefts,
        *rights,
        scratch=[pltpu.VMEM((3 * GROUP, width), F32)] * 2,
    )[0]
    sums = lax.all_to_all(parts, AXES, 0, 0, tiled=True)
    sums = jnp.pad(sums, ((0, -count % 8), (0, 0)))
    sol, res, norms = local_call(finish_body, [row, row, (1, 3)], sums, *lefts, *rights)
    return sol.reshape(width), res.reshape(width), norms.reshape(3)


def solution(mesh):
    assert mesh.shape["sub"] == 2
    both = P(AXES)
    wide = P(AXES, None)
    return jax.shard_map(
        per_device,
        mesh=mesh,
        in_specs=(both, both, wide, wide, wide, wide, P("dom", None), P("dom")),
        out_specs=(both, both, P()),
        check_vma=False,
    )
```

time: 229 us -> 75.5 us (0.33)
  blocking collectives: 150 us -> 18.6 us
  between operations: 10.8 us -> 0.86 us
  matrix products: 8.57 us -> 0 us
  Pallas kernels: 0 us -> 6.94 us
  other arithmetic: 6.91 us -> 0 us
  starting transfers between devices: 45.3 us -> 38.9 us
  waiting for transfers between devices: 3.15 us -> 5.61 us
    psum x3 -> x0, blocking collectives: 138 us -> none  [three_sums(): lax.psum((jnp.sum(resid * uvec), jnp.sum(wvec * uvec), jnp.sum(resid * re...]
    all_to_all x0 -> x1, blocking collectives: none -> 18.6 us  [per_device(): sums = lax.all_to_all(parts, AXES, 0, 0, tiled=True)]
    all_gather x3 -> x0, blocking collectives: 12.2 us -> none  [precond(): eboth = lax.all_gather(eone, 'sub', axis=0, tiled=True)]
    dot_general x36 -> x0, matrix products: 8.57 us -> none  [the longest x9 2.78 us: apply(): jnp.dot(selfm, vec, precision=HIGH) + jnp.dot(coup, upper, precision=HIGH)]
    pallas_call x0 -> x24, Pallas kernels: none -> 6.94 us  [local_call(): pl.pallas_call(body, out_shape=[jax.ShapeDtypeStruct(s, F32) for s in out...]
    ppermute x18 -> x15, starting transfers between devices: 45.3 us -> 38.9 us  [move(): return lax.ppermute(value, AXES, pairs)]
    ppermute x18 -> x15, waiting for transfers between devices: 3.15 us -> 5.61 us  [move(): return lax.ppermute(value, AXES, pairs)]
    another operation x1 -> x0, other arithmetic: 2.41 us -> none  [per_device(): return (solution, resid, jnp.stack(norm_list))]
  transfers between devices with their start and end apart: 18 -> 15, of which waited for: 6 -> 7; matrix products, arithmetic and copies ran while one was open for 4% -> 0% of each run, Pallas kernels for 0% -> 2%
where the time goes in v2:
time: 75.5 us; the launch traced here: 75.1 us
  starting transfers between devices  38.9 us (52%)
  blocking collectives  18.6 us (25%)
  Pallas kernels  6.94 us (9%)
  waiting for transfers between devices  5.61 us (7%)
  local copies, waits for them, and re-layouts  4.23 us (6%)
  between operations  0.86 us (1%)
    ppermute x15, starting transfers between devices, move(): return lax.ppermute(value, AXES, pairs)  38.9 us
    all_to_all x1, blocking collectives, per_device(): sums = lax.all_to_all(parts, AXES, 0, 0, tiled=True)  18.6 us
    pallas_call x24, Pallas kernels, local_call(): pl.pallas_call(body, out_shape=[jax.ShapeDtypeStruct(s, F32) for s in out...  6.94 us
    ppermute x15, waiting for transfers between devices, move(): return lax.ppermute(value, AXES, pairs)  5.61 us
    unnamed x16, local copies, waits for them, and re-layouts  4.23 us
  transfers between devices with their start and end apart: 15, of which 7 were waited for; matrix products, arithmetic and copies ran while one was open for 0% of the time, Pallas kernels for 2%

profile of v2, /device:TPU:0, one launch (start us, length us, event | category | flops | bytes accessed | tf_op | source)
XLA Modules:
  0.0 75.1 jit_solution(6761281211619342280)
XLA Ops:
  1.3 0.9 %copy-done.3 = f32[256,256]{1,0:T(8,128)S(1)} copy-done((f32[256,256]{1,0:T(8,128)S(1)}, f32[256,256]{1,0:T(8,128)}, u32[]{:S(2)}) %copy-start.3) | copy-done | bytes 262168
  2.3 0.8 %shard_map.103 = (f32[256,256]{1,0:T(8,128)S(1)}, f32[3,256]{1,0:T(4,128)S(1)}) custom-call(f32[1,256]{1,0:T(1,128)S(1)} %bitcast.12, f32[1,256]{1,0:T(1,128)S(1)} %bitcast.16, f32[256,256]{1,0:T(8,128)S(1)} %copy-done.3, s32[2,2]{1,0:T(2,128)S(1)} %copy-done.6), custom_call_target="tpu_custom_call" | custom-call | flops 200000 | bytes 1000 | tf_op jit(solution)/shard_map/pallas_call | solution.py:19
  3.8 0.9 %copy-done.1 = f32[256,256]{1,0:T(8,128)S(1)} copy-done((f32[256,256]{1,0:T(8,128)S(1)}, f32[256,256]{1,0:T(8,128)}, u32[]{:S(2)}) %copy-start.1) | copy-done | bytes 262168
  4.7 0.9 %copy-done.2 = f32[256,256]{1,0:T(8,128)S(1)} copy-done((f32[256,256]{1,0:T(8,128)S(1)}, f32[256,256]{1,0:T(8,128)}, u32[]{:S(2)}) %copy-start.2) | copy-done | bytes 262168
  6.6 0.7 collective-permute-start.5
  7.3 0.7 collective-permute-start.1
  8.0 5.2 %collective-permute-start = (f32[3,256]{1,0:T(4,128)S(1)}, f32[3,256]{1,0:T(4,128)S(1)}, u32[]{:S(2)}, u32[]{:S(2)}) collective-permute-start(f32[3,256]{1,0:T(4,128)S(1)} %get-tuple-element.21.sent), channel_id=1, source_target_pairs={{0,1},{1,0},{2,3},{3,2},{4,5},{5,4},{6,7},{7,6},{8,9},{9,8},{10,11... | collective-permute-start | bytes 9224 | tf_op jit(solution)/shard_map/ppermute | solution.py:331
  13.2 0.8 %collective-permute-done.inner = f32[3,256]{1,0:T(4,128)S(1)} collective-permute-done((f32[3,256]{1,0:T(4,128)S(1)}, f32[3,256]{1,0:T(4,128)S(1)}, u32[]{:S(2)}, u32[]{:S(2)}) %collective-permute-start) | collective-permute-done | bytes 3104 | tf_op jit(solution)/shard_map/ppermute | solution.py:331
  14.1 2.2 %collective-permute-start.2 = (f32[1,128]{1,0:T(1,128)S(1)}, f32[1,128]{1,0:T(1,128)S(1)}, u32[]{:S(2)}, u32[]{:S(2)}) collective-permute-start(f32[1,128]{1,0:T(1,128)S(1)} %shard_map.105.ca), channel_id=1, source_target_pairs={{0,1},{1,0},{2,3},{3,2},{4,5},{5,4},{6,7},{7,6},{8,9},{9,8},{10,11... | collective-permute-start | bytes 1544 | tf_op jit(solution)/shard_map/ppermute | solution.py:331
  16.5 0.7 collective-permute-done.2.cb
  18.5 4.7 %collective-permute-start.6 = (f32[2,256]{1,0:T(2,128)S(1)}, f32[2,256]{1,0:T(2,128)S(1)}, u32[]{:S(2)}, u32[]{:S(2)}) collective-permute-start(f32[2,256]{1,0:T(2,128)S(1)} %shard_map.111.sent.refs_4_.u0), channel_id=1, source_target_pairs={{0,1},{1,0},{2,3},{3,2},{4,5},{5,4},{6,7},{7,6},{8,9},{9,8},{10,11... | collective-permute-start | bytes 6152 | tf_op jit(solution)/shard_map/ppermute | solution.py:331
  23.3 0.8 %collective-permute-done.6.got = f32[2,256]{1,0:T(2,128)S(1)} collective-permute-done((f32[2,256]{1,0:T(2,128)S(1)}, f32[2,256]{1,0:T(2,128)S(1)}, u32[]{:S(2)}, u32[]{:S(2)}) %collective-permute-start.6) | collective-permute-done | bytes 2080 | tf_op jit(solution)/shard_map/ppermute | solution.py:331
  25.2 5.4 %collective-permute-start.8 = (f32[1,128]{1,0:T(1,128)S(1)}, f32[1,128]{1,0:T(1,128)S(1)}, u32[]{:S(2)}, u32[]{:S(2)}) collective-permute-start(f32[1,128]{1,0:T(1,128)S(1)} %shard_map.114.ca), channel_id=1, source_target_pairs={{0,1},{1,0},{2,3},{3,2},{4,5},{5,4},{6,7},{7,6},{8,9},{9,8},{10,11... | collective-permute-start | bytes 1544 | tf_op jit(solution)/shard_map/ppermute | solution.py:331
  30.6 0.8 %collective-permute-done.8.cb = f32[1,128]{1,0:T(1,128)S(1)} collective-permute-done((f32[1,128]{1,0:T(1,128)S(1)}, f32[1,128]{1,0:T(1,128)S(1)}, u32[]{:S(2)}, u32[]{:S(2)}) %collective-permute-start.8) | collective-permute-done | bytes 544 | tf_op jit(solution)/shard_map/ppermute | solution.py:331
  32.6 5.4 %collective-permute-start.10 = (f32[2,256]{1,0:T(2,128)S(1)}, f32[2,256]{1,0:T(2,128)S(1)}, u32[]{:S(2)}, u32[]{:S(2)}) collective-permute-start(f32[2,256]{1,0:T(2,128)S(1)} %shard_map.117.sent.refs_5_.m0), channel_id=1, source_target_pairs={{0,1},{1,0},{2,3},{3,2},{4,5},{5,4},{6,7},{7,6},{8,9},{9,8},{10,11... | collective-permute-start | bytes 6152 | tf_op jit(solution)/shard_map/ppermute | solution.py:331
  38.0 0.8 %collective-permute-done.10.got = f32[2,256]{1,0:T(2,128)S(1)} collective-permute-done((f32[2,256]{1,0:T(2,128)S(1)}, f32[2,256]{1,0:T(2,128)S(1)}, u32[]{:S(2)}, u32[]{:S(2)}) %collective-permute-start.10) | collective-permute-done | bytes 2080 | tf_op jit(solution)/shard_map/ppermute | solution.py:331
  39.9 5.4 %collective-permute-start.12 = (f32[1,128]{1,0:T(1,128)S(1)}, f32[1,128]{1,0:T(1,128)S(1)}, u32[]{:S(2)}, u32[]{:S(2)}) collective-permute-start(f32[1,128]{1,0:T(1,128)S(1)} %shard_map.120.ca), channel_id=1, source_target_pairs={{0,1},{1,0},{2,3},{3,2},{4,5},{5,4},{6,7},{7,6},{8,9},{9,8},{10,11... | collective-permute-start | bytes 1544 | tf_op jit(solution)/shard_map/ppermute | solution.py:331
  45.3 0.8 %collective-permute-done.12.cb = f32[1,128]{1,0:T(1,128)S(1)} collective-permute-done((f32[1,128]{1,0:T(1,128)S(1)}, f32[1,128]{1,0:T(1,128)S(1)}, u32[]{:S(2)}, u32[]{:S(2)}) %collective-permute-start.12) | collective-permute-done | bytes 544 | tf_op jit(solution)/shard_map/ppermute | solution.py:331
  47.3 5.4 %collective-permute-start.14 = (f32[2,256]{1,0:T(2,128)S(1)}, f32[2,256]{1,0:T(2,128)S(1)}, u32[]{:S(2)}, u32[]{:S(2)}) collective-permute-start(f32[2,256]{1,0:T(2,128)S(1)} %shard_map.123.sent.refs_6_.m1), channel_id=1, source_target_pairs={{0,1},{1,0},{2,3},{3,2},{4,5},{5,4},{6,7},{7,6},{8,9},{9,8},{10,11... | collective-permute-start | bytes 6152 | tf_op jit(solution)/shard_map/ppermute | solution.py:331
  52.7 0.8 %collective-permute-done.14.got = f32[2,256]{1,0:T(2,128)S(1)} collective-permute-done((f32[2,256]{1,0:T(2,128)S(1)}, f32[2,256]{1,0:T(2,128)S(1)}, u32[]{:S(2)}, u32[]{:S(2)}) %collective-permute-start.14) | collective-permute-done | bytes 2080 | tf_op jit(solution)/shard_map/ppermute | solution.py:331
  53.6 0.7 shard_map.124
  54.3 0.7 shard_map.125
  55.0 18.6 %all_to_all.11 = f32[32,1,128]{2,1,0:T(1,128)S(1)} all-to-all(f32[32,1,128]{2,1,0:T(1,128)S(1)} %bitcast.11), channel_id=1, replica_groups=mesh['dom'=16,'sub'=2] {'dom','sub'}, dimensions={0} | all-to-all | bytes 32768 | tf_op jit(solution)/shard_map/all_to_all | solution.py:389
  73.5 1.6 %shard_map.126 = (f32[1,256]{1,0:T(1,128)}, f32[1,256]{1,0:T(1,128)}, f32[1,3]{1,0:T(1,128)}) custom-call(f32[32,128]{1,0:T(8,128)S(1)} %bitcast.10, f32[1,256]{1,0:T(1,128)S(1)} %bitcast.15, f32[3,256]{1,0:T(4,128)S(1)} %get-tuple-element.31.state.refs_1_.w0, f32[3,256]{1,0:T(4,128)S(1)} %get-tuple-element.33.state.refs_2_.n0, ...), custom_call_target="tpu_custom_call" | custom-call | flops 200000 | bytes 1000 | tf_op jit(solution)/shard_map/pallas_call | solution.py:19
  (47 shorter events, 8.5 us)
Async XLA Ops:
  0.6 0.7 copy-start.5
  0.6 0.7 copy-start.6
  0.7 0.7 copy-start.4
  1.3 0.9 %copy-start.3 = (f32[256,256]{1,0:T(8,128)S(1)}, f32[256,256]{1,0:T(8,128)}, u32[]{:S(2)}) copy-start(f32[256,256]{1,0:T(8,128)} %coup.1) | copy-start | bytes 786436
  2.3 0.9 %copy-start = (f32[256,128]{1,0:T(8,128)S(1)}, f32[256,128]{1,0:T(8,128)}, u32[]{:S(2)}) copy-start(f32[256,128]{1,0:T(8,128)} %pro.11) | copy-start | bytes 393220
  3.1 0.7 copy-start.7
  3.8 0.9 %copy-start.1 = (f32[256,256]{1,0:T(8,128)S(1)}, f32[256,256]{1,0:T(8,128)}, u32[]{:S(2)}) copy-start(f32[256,256]{1,0:T(8,128)} %raw.1) | copy-start | bytes 786436
  4.7 0.9 %copy-start.2 = (f32[256,256]{1,0:T(8,128)S(1)}, f32[256,256]{1,0:T(8,128)}, u32[]{:S(2)}) copy-start(f32[256,256]{1,0:T(8,128)} %craw.1) | copy-start | bytes 786436
  6.1 10.3 %collective-permute-start.3 = (f32[640,256]{1,0:T(8,128)S(1)}, f32[640,256]{1,0:T(8,128)S(1)}, u32[]{:S(2)}, u32[]{:S(2)}) collective-permute-start(f32[640,256]{1,0:T(8,128)S(1)} %get-tuple-element.23.packed), channel_id=1, source_target_pairs={{0,1},{1,0},{2,3},{3,2},{4,5},{5,4},{6,7},{7,6},{8,9},{9,8},{10,11... | collective-permute-start | bytes 1966088 | tf_op jit(solution)/shard_map/ppermute | solution.py:331
  6.6 11.4 %collective-permute-start.5 = (f32[256,256]{1,0:T(8,128)S(1)}, f32[256,256]{1,0:T(8,128)S(1)}, u32[]{:S(2)}, u32[]{:S(2)}) collective-permute-start(f32[256,256]{1,0:T(8,128)S(1)} %get-tuple-element.22.cm), channel_id=1, source_target_pairs={{1,2},{3,4},{5,6},{7,8},{9,10},{11,12},{13,14},{15,16},{17,18},{19... | collective-permute-start | bytes 786440 | tf_op jit(solution)/shard_map/ppermute | solution.py:331
  7.3 5.8 %collective-permute-start.1 = (f32[3,256]{1,0:T(4,128)S(1)}, f32[3,256]{1,0:T(4,128)S(1)}, u32[]{:S(2)}, u32[]{:S(2)}) collective-permute-start(f32[3,256]{1,0:T(4,128)S(1)} %get-tuple-element.21.sent), channel_id=1, source_target_pairs={{1,2},{3,4},{5,6},{7,8},{9,10},{11,12},{13,14},{15,16},{17,18},{19... | collective-permute-start | bytes 9224 | tf_op jit(solution)/shard_map/ppermute | solution.py:331
  8.0 6.0 %collective-permute-start = (f32[3,256]{1,0:T(4,128)S(1)}, f32[3,256]{1,0:T(4,128)S(1)}, u32[]{:S(2)}, u32[]{:S(2)}) collective-permute-start(f32[3,256]{1,0:T(4,128)S(1)} %get-tuple-element.21.sent), channel_id=1, source_target_pairs={{0,1},{1,0},{2,3},{3,2},{4,5},{5,4},{6,7},{7,6},{8,9},{9,8},{10,11... | collective-permute-start | bytes 9224 | tf_op jit(solution)/shard_map/ppermute | solution.py:331
  14.1 3.0 %collective-permute-start.2 = (f32[1,128]{1,0:T(1,128)S(1)}, f32[1,128]{1,0:T(1,128)S(1)}, u32[]{:S(2)}, u32[]{:S(2)}) collective-permute-start(f32[1,128]{1,0:T(1,128)S(1)} %shard_map.105.ca), channel_id=1, source_target_pairs={{0,1},{1,0},{2,3},{3,2},{4,5},{5,4},{6,7},{7,6},{8,9},{9,8},{10,11... | collective-permute-start | bytes 1544 | tf_op jit(solution)/shard_map/ppermute | solution.py:331
  17.4 1.0 %collective-permute-start.4 = (f32[2,256]{1,0:T(2,128)S(1)}, f32[2,256]{1,0:T(2,128)S(1)}, u32[]{:S(2)}, u32[]{:S(2)}) collective-permute-start(f32[2,256]{1,0:T(2,128)S(1)} %shard_map.108.sent), channel_id=1, source_target_pairs={{1,2},{3,4},{5,6},{7,8},{9,10},{11,12},{13,14},{15,16},{17,18},{19... | collective-permute-start | bytes 6152 | tf_op jit(solution)/shard_map/ppermute | solution.py:331
  18.5 5.6 %collective-permute-start.6 = (f32[2,256]{1,0:T(2,128)S(1)}, f32[2,256]{1,0:T(2,128)S(1)}, u32[]{:S(2)}, u32[]{:S(2)}) collective-permute-start(f32[2,256]{1,0:T(2,128)S(1)} %shard_map.111.sent.refs_4_.u0), channel_id=1, source_target_pairs={{0,1},{1,0},{2,3},{3,2},{4,5},{5,4},{6,7},{7,6},{8,9},{9,8},{10,11... | collective-permute-start | bytes 6152 | tf_op jit(solution)/shard_map/ppermute | solution.py:331
  24.2 0.8 %collective-permute-start.7 = (f32[1,256]{1,0:T(1,128)S(1)}, f32[1,256]{1,0:T(1,128)S(1)}, u32[]{:S(2)}, u32[]{:S(2)}) collective-permute-start(f32[1,256]{1,0:T(1,128)S(1)} %get-tuple-element.32), channel_id=1, source_target_pairs={{1,2},{3,4},{5,6},{7,8},{9,10},{11,12},{13,14},{15,16},{17,18},{19... | collective-permute-start | bytes 3080 | tf_op jit(solution)/shard_map/ppermute | solution.py:331
  25.2 6.2 %collective-permute-start.8 = (f32[1,128]{1,0:T(1,128)S(1)}, f32[1,128]{1,0:T(1,128)S(1)}, u32[]{:S(2)}, u32[]{:S(2)}) collective-permute-start(f32[1,128]{1,0:T(1,128)S(1)} %shard_map.114.ca), channel_id=1, source_target_pairs={{0,1},{1,0},{2,3},{3,2},{4,5},{5,4},{6,7},{7,6},{8,9},{9,8},{10,11... | collective-permute-start | bytes 1544 | tf_op jit(solution)/shard_map/ppermute | solution.py:331
  31.6 0.8 %collective-permute-start.9 = (f32[2,256]{1,0:T(2,128)S(1)}, f32[2,256]{1,0:T(2,128)S(1)}, u32[]{:S(2)}, u32[]{:S(2)}) collective-permute-start(f32[2,256]{1,0:T(2,128)S(1)} %shard_map.115.sent), channel_id=1, source_target_pairs={{1,2},{3,4},{5,6},{7,8},{9,10},{11,12},{13,14},{15,16},{17,18},{19... | collective-permute-start | bytes 6152 | tf_op jit(solution)/shard_map/ppermute | solution.py:331
  32.6 6.2 %collective-permute-start.10 = (f32[2,256]{1,0:T(2,128)S(1)}, f32[2,256]{1,0:T(2,128)S(1)}, u32[]{:S(2)}, u32[]{:S(2)}) collective-permute-start(f32[2,256]{1,0:T(2,128)S(1)} %shard_map.117.sent.refs_5_.m0), channel_id=1, source_target_pairs={{0,1},{1,0},{2,3},{3,2},{4,5},{5,4},{6,7},{7,6},{8,9},{9,8},{10,11... | collective-permute-start | bytes 6152 | tf_op jit(solution)/shard_map/ppermute | solution.py:331
  39.0 0.8 %collective-permute-start.11 = (f32[1,256]{1,0:T(1,128)S(1)}, f32[1,256]{1,0:T(1,128)S(1)}, u32[]{:S(2)}, u32[]{:S(2)}) collective-permute-start(f32[1,256]{1,0:T(1,128)S(1)} %get-tuple-element.34), channel_id=1, source_target_pairs={{1,2},{3,4},{5,6},{7,8},{9,10},{11,12},{13,14},{15,16},{17,18},{19... | collective-permute-start | bytes 3080 | tf_op jit(solution)/shard_map/ppermute | solution.py:331
  39.9 6.2 %collective-permute-start.12 = (f32[1,128]{1,0:T(1,128)S(1)}, f32[1,128]{1,0:T(1,128)S(1)}, u32[]{:S(2)}, u32[]{:S(2)}) collective-permute-start(f32[1,128]{1,0:T(1,128)S(1)} %shard_map.120.ca), channel_id=1, source_target_pairs={{0,1},{1,0},{2,3},{3,2},{4,5},{5,4},{6,7},{7,6},{8,9},{9,8},{10,11... | collective-permute-start | bytes 1544 | tf_op jit(solution)/shard_map/ppermute | solution.py:331
  46.4 0.8 %collective-permute-start.13 = (f32[2,256]{1,0:T(2,128)S(1)}, f32[2,256]{1,0:T(2,128)S(1)}, u32[]{:S(2)}, u32[]{:S(2)}) collective-permute-start(f32[2,256]{1,0:T(2,128)S(1)} %shard_map.121.sent), channel_id=1, source_target_pairs={{1,2},{3,4},{5,6},{7,8},{9,10},{11,12},{13,14},{15,16},{17,18},{19... | collective-permute-start | bytes 6152 | tf_op jit(solution)/shard_map/ppermute | solution.py:331
  47.3 6.2 %collective-permute-start.14 = (f32[2,256]{1,0:T(2,128)S(1)}, f32[2,256]{1,0:T(2,128)S(1)}, u32[]{:S(2)}, u32[]{:S(2)}) collective-permute-start(f32[2,256]{1,0:T(2,128)S(1)} %shard_map.123.sent.refs_6_.m1), channel_id=1, source_target_pairs={{0,1},{1,0},{2,3},{3,2},{4,5},{5,4},{6,7},{7,6},{8,9},{9,8},{10,11... | collective-permute-start | bytes 6152 | tf_op jit(solution)/shard_map/ppermute | solution.py:331

commit v3 on v2

v3 whole, which is shorter than its diff:
```python
import functools

import jax
import jax.numpy as jnp
from jax import lax
from jax.experimental import pallas as pl
from jax.experimental.pallas import tpu as pltpu
from jax.sharding import PartitionSpec as P

AXES = ("dom", "sub")
OMEGA = 0.7
LANES = 128
GROUP = 16
F32 = jnp.float32


def local_call(body, outs, *args, hbm=0, scratch=(), flops=200_000):
    spaces = [pltpu.HBM if i < hbm else pltpu.VMEM for i in range(len(args))]
    args = [pltpu.with_memory_space_constraint(a, pltpu.HBM) for a in args[:hbm]] + list(args[hbm:])
    return pl.pallas_call(
        body,
        out_shape=[jax.ShapeDtypeStruct(s, F32) for s in outs],
        in_specs=[pl.BlockSpec(memory_space=s) for s in spaces],
        out_specs=[pl.BlockSpec(memory_space=pltpu.VMEM) for _ in outs],
        scratch_shapes=list(scratch),
        cost_estimate=pl.CostEstimate(flops=flops, bytes_accessed=1000, transcendentals=0),
        compiler_params=pltpu.CompilerParams(vmem_limit_bytes=8 * 1024 * 1024),
    )(*args)


def unit(rows, cols):
    shape = (rows, cols)
    return lax.broadcasted_iota(jnp.int32, shape, 0) == lax.broadcasted_iota(jnp.int32, shape, 1)


def over_lanes(a):
    return jnp.sum(a, axis=1, keepdims=True)


def over_rows(a):
    return jnp.sum(a, axis=0, keepdims=True)


def as_row(col):
    eye = unit(LANES, LANES)
    pieces = [
        over_rows(jnp.where(eye, col[k : k + LANES], 0.0)) for k in range(0, col.shape[0], LANES)
    ]
    return jnp.concatenate(pieces, axis=1)


def as_col(row):
    eye = unit(LANES, LANES)
    pieces = [
        over_lanes(jnp.where(eye, row[:, k : k + LANES], 0.0))
        for k in range(0, row.shape[1], LANES)
    ]
    return jnp.concatenate(pieces, axis=0)


def two_sum(a, b):
    s = a + b
    t = s - a
    return s, (a - (s - t)) + (b - t)


def halves(a):
    t = 4097.0 * a
    hi = t - (t - a)
    return hi, a - hi


def two_prod(a, b):
    p = a * b
    ah, al = halves(a)
    bh, bl = halves(b)
    return p, ((ah * bh - p) + ah * bl + al * bh) + al * bl


def pair_add(a, b):
    s, e = two_sum(a[0], b[0])
    e = e + (a[1] + b[1])
    hi = s + e
    return hi, e - (hi - s)


def pair_mul(a, b):
    p, e = two_prod(a[0], b[0])
    e = e + (a[0] * b[1] + a[1] * b[0])
    hi = p + e
    return hi, e - (hi - p)


def fetch(sources, targets, sems):
    copies = [pltpu.make_async_copy(*pair, sems.at[k]) for k, pair in enumerate(zip(sources, targets))]
    for copy in copies:
        copy.start()
    return copies


def start_body(rhs_h, diag_h, pattern_h, coup_h, cm, sent, rhs, diag, pattern, coup, sems):
    for copy in fetch((rhs_h, diag_h, pattern_h, coup_h), (rhs, diag, pattern, coup), sems):
        copy.wait()
    blocks = pattern.shape[0]
    step = coup.shape[0] // blocks
    for i in range(blocks):
        for j in range(blocks):
            keep = pattern[i : i + 1, j : j + 1].astype(F32)
            rows, cols = pl.ds(i * step, step), pl.ds(j * step, step)
            cm[rows, cols] = coup[rows, cols] * keep
    scale = OMEGA / diag[...]
    first = scale * rhs[...]
    sent[0:1] = over_rows(cm[...] * as_col(first))
    sent[1:2] = first
    sent[2:3] = scale
    sent[3:4] = rhs[...]


def setup_body(
    raw_h, craw_h, cdiag_h, pro_h, sent, cm, packed, fmat, raw, craw, cdiag, pro, sems
):
    width = raw.shape[0]
    coarse = pro.shape[1]
    copies = fetch((raw_h, pro_h, cdiag_h, craw_h), (raw, pro, cdiag, craw), sems)
    packed[width : 2 * width] = cm[...]
    eye = unit(width, width)
    diag = OMEGA / sent[2:3]
    copies[0].wait()
    r = raw[...]
    packed[0:width] = jnp.where(eye, diag * (1.0 - 1.0 / OMEGA), 0.5 * (r + r.T))
    copies[1].wait()
    packed[2 * width :] = pro[...].T
    copies[2].wait()
    copies[3].wait()
    q = craw[...]
    inv = 1.0 / cdiag[...]
    fmat[...] = jnp.where(
        unit(2 * coarse, 2 * coarse), inv, -0.5 * (q + q.T) * inv * as_col(inv)
    )


def parity():
    return lax.axis_index("dom") % 2


def both_ways(even, odd, rightward, leftward):
    is_even = parity() == 0
    even[...] = jnp.where(is_even, rightward, leftward)
    odd[...] = jnp.where(is_even, leftward, rightward)


def from_sides(even, odd):
    dom, last = lax.axis_index("dom"), lax.axis_size("dom") - 1
    is_even = parity() == 0
    e, o = even[...], odd[...]
    left = jnp.where(dom > 0, jnp.where(is_even, o, e), 0.0)
    right = jnp.where(dom < last, jnp.where(is_even, e, o), 0.0)
    return left, right


def pair_body(sent, inner, even, odd, scale, state):
    low = lax.axis_index("sub") == 0
    own, other = sent[...], inner[...]
    left, right = jnp.where(low, own, other), jnp.where(low, other, own)
    both_ways(
        even,
        odd,
        jnp.concatenate([right[0:1], right[2:3]], axis=0),
        left[1:3],
    )
    scale[0:1] = left[2:3]
    scale[1:2] = right[2:3]
    state[0:1] = left[3:4]
    state[1:2] = right[3:4]
    state[2:3] = left[1:2]
    state[3:4] = right[1:2]


def order_body(packed, other, sl, sr, cin, cint, cr, crt, ptl, ptr, prl, prr):
    width = sl.shape[0]

    def place(low, high):
        sl[...] = low[0:width]
        sr[...] = high[0:width]
        c = low[width : 2 * width]
        cin[...] = c
        cint[...] = c.T
        c = high[width : 2 * width]
        cr[...] = c
        crt[...] = c.T
        p = low[2 * width :]
        ptl[...] = p
        prl[...] = p.T
        p = high[2 * width :]
        ptr[...] = p
        prr[...] = p.T

    core = lax.axis_index("sub")

    @pl.when(core == 0)
    def _():
        place(packed, other)

    @pl.when(core != 0)
    def _():
        place(other, packed)


def left_edge_body(up, swapped, cl, clt):
    c = jnp.where(lax.axis_index("sub") == 0, up[...], swapped[...])
    c = jnp.where(lax.axis_index("dom") > 0, c, 0.0)
    cl[...] = c.T
    clt[...] = c


def smooth(c, state, scale, fmat, sl, sr, cin, cint, ptl, ptr, half, even, odd):
    coarse = ptl.shape[0]
    e = over_lanes(fmat[...] * c)
    xl = state[2:3] + over_rows(ptl[...] * e[:coarse])
    xr = state[3:4] + over_rows(ptr[...] * e[coarse:])
    vl = as_row(over_lanes(sl[...] * xl + cin[...] * xr))
    vr = as_row(over_lanes(sr[...] * xr + cint[...] * xl))
    ml = scale[0:1] * (state[0:1] - vl)
    mr = scale[1:2] * (state[1:2] - vr)
    half[0:1] = xl
    half[1:2] = xr
    half[2:3] = ml
    half[3:4] = mr
    both_ways(
        even, odd, jnp.concatenate([xr, mr], axis=0), jnp.concatenate([xl, ml], axis=0)
    )


def first_body(
    goteven, gotodd, state, scale, fmat, sl, sr, cin, cint, cr, ptl, ptr, prl, prr, half, even, odd, outer
):
    width = sl.shape[0]
    left, right = from_sides(goteven, gotodd)
    outer[0:1] = left[1:2]
    outer[1:2] = right[1:2]
    x1l, x1r = state[2:3], state[3:4]
    done = jnp.where(unit(width, width), left[0:1], 0.0)
    rl = over_lanes(sl[...] * x1l + cin[...] * x1r + done)
    rr = over_lanes(sr[...] * x1r + cint[...] * x1l + cr[...] * right[0:1])
    c = jnp.concatenate([over_rows(prl[...] * rl), over_rows(prr[...] * rr)], axis=1)
    smooth(-c, state, scale, fmat, sl, sr, cin, cint, ptl, ptr, half, even, odd)


def restrict_local_body(state, sl, sr, cin, cint, prl, prr, out):
    x1l, x1r = state[2:3], state[3:4]
    rl = over_lanes(sl[...] * x1l + cin[...] * x1r)
    rr = over_lanes(sr[...] * x1r + cint[...] * x1l)
    out[...] = jnp.concatenate([over_rows(prl[...] * rl), over_rows(prr[...] * rr)], axis=1)


def next_body(
    goteven, gotodd, local, state, scale, fmat, sl, sr, cin, cint, cl, cr, ptl, ptr, prl, prr, half, even, odd
):
    left, right = from_sides(goteven, gotodd)
    rl = over_lanes(cl[...] * left)
    rr = over_lanes(cr[...] * right)
    c = jnp.concatenate([over_rows(prl[...] * rl), over_rows(prr[...] * rr)], axis=1)
    smooth(-(local[...] + c), state, scale, fmat, sl, sr, cin, cint, ptl, ptr, half, even, odd)


def edge_local_body(half, outer, clt, crt, out):
    out[0:1] = outer[0:1] * as_row(over_lanes(clt[...] * half[0:1]))
    out[1:2] = outer[1:2] * as_row(over_lanes(crt[...] * half[1:2]))


def apply_body(
    goteven, gotodd, half, owed, scale, sl, sr, cin, cint, cl, cr, state, even, odd, own
):
    left, right = from_sides(goteven, gotodd)
    ml = half[2:3] - scale[0:1] * as_row(over_lanes(cl[...] * left[0:1]))
    mr = half[3:4] - scale[1:2] * as_row(over_lanes(cr[...] * right[0:1]))
    mol = left[1:2] - owed[0:1]
    mor = right[1:2] - owed[1:2]
    nl = as_row(over_lanes(sl[...] * ml + cin[...] * mr + cl[...] * mol)) + ml / scale[0:1]
    nr = as_row(over_lanes(sr[...] * mr + cint[...] * ml + cr[...] * mor)) + mr / scale[1:2]
    xl, xr = scale[0:1] * nl, scale[1:2] * nr
    state[0:1] = nl
    state[1:2] = nr
    state[2:3] = xl
    state[3:4] = xr
    both_ways(even, odd, xr, xl)
    low = lax.axis_index("sub") == 0
    own[0:1] = jnp.where(low, nl, nr)
    own[1:2] = jnp.where(low, ml, mr)


def basis(sent, *owns):
    return [sent[3:4]] + [own[0:1] for own in owns], [own[1:2] for own in owns]


def gram_body(sent, own0, own1, own2, out, xs, ys):
    lefts, rights = basis(sent, own0, own1, own2)
    xs[...] = jnp.zeros_like(xs)
    ys[...] = jnp.zeros_like(ys)
    for i in range(3):
        for j in range(3):
            for group, a, b in (
                (0, lefts[i], rights[j]),
                (1, lefts[i + 1], rights[j]),
                (2, lefts[i], lefts[j]),
            ):
                at = group * GROUP + 3 * i + j
                xs[at : at + 1] = a
                ys[at : at + 1] = b
    hi, lo = two_prod(xs[...], ys[...])
    parts = [(hi[:, k : k + LANES], lo[:, k : k + LANES]) for k in range(0, hi.shape[1], LANES)]
    total = functools.reduce(pair_add, parts)
    step = LANES // 2
    while step:
        total = pair_add(total, tuple(pltpu.roll(t, step, 1) for t in total))
        step //= 2
    eye = unit(xs.shape[0], LANES)
    hi, lo = (over_rows(jnp.where(eye, t, 0.0)) for t in total)
    row = hi + pltpu.roll(jnp.broadcast_to(lo, (8, LANES)), LANES // 2, 1)[0:1]
    out[...] = jnp.broadcast_to(row, out.shape)


def finish_body(got, sent, own0, own1, own2, sol, res, norms):
    full = got[...]
    rows = full.shape[0]
    tiles = [full[k : k + 8] for k in range(0, rows, 8)]
    pairs = [(t, pltpu.roll(t, LANES // 2, 1)) for t in tiles]
    while len(pairs) > 1:
        rest = pairs[len(pairs) // 2 * 2 :]
        pairs = [pair_add(pairs[k], pairs[k + 1]) for k in range(0, len(pairs) - 1, 2)] + rest
    gram = pairs[0]
    for step in (4, 2, 1):
        gram = pair_add(gram, tuple(pltpu.roll(t, step, 0) for t in gram))
    lane = lax.broadcasted_iota(jnp.int32, (8, LANES), 1)
    term = lane % GROUP
    left, right = term // 3, term % 3
    valid = (term < 9) & (lane < 3 * GROUP)
    gram = tuple(jnp.where(valid, t, 0.0) for t in gram)

    def at(value, where):
        return over_lanes(jnp.where(lane == where, value, 0.0))

    def form(c1, c2):
        def coefficient(index):
            hi = jnp.where(index == 0, 1.0, jnp.where(index == 1, -c1[0], c2[0]))
            lo = jnp.where(index == 0, 0.0, jnp.where(index == 1, -c1[1], c2[1]))
            return hi, lo

        total = pair_mul(pair_mul(coefficient(left), coefficient(right)), gram)
        for step in (8, 4, 2, 1):
            total = pair_add(total, tuple(pltpu.roll(t, LANES - step, 1) for t in total))
        return tuple(at(total[0], g * GROUP) for g in range(3))

    gamma0, delta0, rho0 = (at(gram[0], g * GROUP) for g in range(3))
    zero = jnp.zeros_like(gamma0)
    alpha0 = gamma0 / delta0
    gamma1, delta1, rho1 = form((alpha0, zero), (zero, zero))
    beta1 = gamma1 / gamma0
    alpha1 = gamma1 / (delta1 - beta1 * gamma1 / alpha0)
    c1 = pair_add((alpha0, zero), pair_mul((alpha1, zero), two_sum(zero + 1.0, beta1)))
    gamma2, delta2, rho2 = form(c1, two_prod(alpha0, alpha1))
    beta2 = gamma2 / gamma1
    alpha2 = gamma2 / (delta2 - beta2 * gamma2 / alpha1)

    a0, a1, a2, b1, b2 = (t[0:1] for t in (alpha0, alpha1, alpha2, beta1, beta2))
    (rb, rw0, rn0, rn1), (ru0, rm0, rm1) = basis(sent, own0, own1, own2)
    r1 = rb - a0 * rw0
    u1 = ru0 - a0 * rm0
    w1 = rw0 - a0 * rn0
    s1 = w1 + b1 * rw0
    p1 = u1 + b1 * ru0
    z1 = (rn0 - a0 * rn1) + b1 * rn0
    q1 = (rm0 - a0 * rm1) + b1 * rm0
    r2 = r1 - a1 * s1
    u2 = u1 - a1 * q1
    w2 = w1 - a1 * z1
    s2 = w2 + b2 * s1
    p2 = u2 + b2 * p1
    sol[...] = a0 * ru0 + a1 * p1 + a2 * p2
    res[...] = r2 - a2 * s2
    where = lane[0:1]
    row = jnp.where(where == 0, rho0[0:1], jnp.where(where == 1, rho1[0:1], rho2[0:1]))
    norms[...] = row[:, :3]


def exchange_pairs(chips, first):
    pairs = [(2 * g + 1, 2 * g + 2) for g in range(first, chips - 1, 2)]
    used = {p for pair in pairs for p in pair}
    idle = [p for p in range(2 * chips) if p not in used]
    pairs += [(idle[k], idle[k + 1]) for k in range(0, len(idle), 2)]
    return pairs + [(b, a) for a, b in pairs]


def vmem(*shape, dtype=F32):
    return pltpu.VMEM(shape, dtype)


def per_device(rhs, diagonal, self_raw, coupling, pattern, prolong, coarse_raw, coarse_diagonal):
    width, coarse = rhs.shape[0], prolong.shape[1]
    chips = lax.axis_size("dom")
    count = 2 * chips
    inner = [(p, p + 1 - 2 * (p % 2)) for p in range(count)]
    up = [(p, (p + 1) % count) for p in range(count)]
    evens, odds = exchange_pairs(chips, 0), exchange_pairs(chips, 1)
    square, row = (width, width), (1, width)

    def move(value, pairs):
        return lax.ppermute(value, AXES, pairs)

    def exchange(even, odd):
        return move(even, evens), move(odd, odds)

    cm, sent = local_call(
        start_body,
        [square, (4, width)],
        rhs.reshape(row),
        diagonal.reshape(row),
        pattern,
        coupling,
        hbm=4,
        scratch=[
            vmem(*row),
            vmem(*row),
            vmem(*pattern.shape, dtype=pattern.dtype),
            vmem(*square),
            pltpu.SemaphoreType.DMA((4,)),
        ],
    )
    from_inner = move(sent, inner)
    even, odd, scale, state = local_call(
        pair_body, [(2, width), (2, width), (2, width), (4, width)], sent, from_inner
    )
    goteven, gotodd = exchange(even, odd)
    packed, fmat = local_call(
        setup_body,
        [(2 * width + coarse, width), (2 * coarse, 2 * coarse)],
        self_raw,
        coarse_raw,
        coarse_diagonal.reshape(1, 2 * coarse),
        prolong,
        sent,
        cm,
        hbm=4,
        scratch=[
            vmem(*square),
            vmem(2 * coarse, 2 * coarse),
            vmem(1, 2 * coarse),
            vmem(width, coarse),
            pltpu.SemaphoreType.DMA((4,)),
        ],
        flops=100_000_000,
    )
    other = move(packed, inner)
    cm_up = move(cm, up)
    cm_swapped = move(cm_up, inner)
    sl, sr, cin, cint, cr, crt, ptl, ptr, prl, prr = local_call(
        order_body, [square] * 6 + [(coarse, width)] * 2 + [(width, coarse)] * 2, packed, other
    )
    cl, clt = local_call(left_edge_body, [square, square], cm_up, cm_swapped)

    owns = []
    for cycle in range(3):
        if cycle == 0:
            half, even, odd, outer = local_call(
                first_body,
                [(4, width), (2, width), (2, width), (2, width)],
                *(goteven, gotodd, state, scale, fmat),
                *(sl, sr, cin, cint, cr, ptl, ptr, prl, prr),
            )
        else:
            local = local_call(
                restrict_local_body, [(1, 2 * coarse)], state, sl, sr, cin, cint, prl, prr
            )[0]
            half, even, odd = local_call(
                next_body,
                [(4, width), (2, width), (2, width)],
                *(goteven, gotodd, local, state, scale, fmat),
                *(sl, sr, cin, cint, cl, cr, ptl, ptr, prl, prr),
            )
        goteven, gotodd = exchange(even, odd)
        owed = local_call(edge_local_body, [(2, width)], half, outer, clt, crt)[0]
        state, even, odd, own = local_call(
            apply_body,
            [(4, width), row, row, (2, width)],
            *(goteven, gotodd, half, owed, scale, sl, sr, cin, cint, cl, cr),
        )
        owns.append(own)
        if cycle < 2:
            goteven, gotodd = exchange(even, odd)

    parts = local_call(
        gram_body, [(count, LANES)], sent, *owns, scratch=[vmem(3 * GROUP, width)] * 2
    )[0]
    sums = lax.all_to_all(parts, AXES, 0, 0, tiled=True)
    sums = jnp.pad(sums, ((0, -count % 8), (0, 0)))
    sol, res, norms = local_call(finish_body, [row, row, (1, 3)], sums, sent, *owns)
    return sol.reshape(width), res.reshape(width), norms.reshape(3)


def solution(mesh):
    assert mesh.shape["sub"] == 2
    both = P(AXES)
    wide = P(AXES, None)
    return jax.shard_map(
        per_device,
        mesh=mesh,
        in_specs=(both, both, wide, wide, wide, wide, P("dom", None), P("dom")),
        out_specs=(both, both, P()),
        check_vma=False,
    )
```

time: 75.5 us -> 62.3 us (0.83)
  starting transfers between devices: 38.9 us -> 18.2 us
  waiting for transfers between devices: 5.61 us -> 19 us
  local copies, waits for them, and re-layouts: 4.23 us -> 0 us
  blocking collectives: 18.6 us -> 15 us
  Pallas kernels: 6.94 us -> 9.22 us
    ppermute x15 -> x16, starting transfers between devices: 38.9 us -> 18.2 us  [move(): return lax.ppermute(value, AXES, pairs)]
    ppermute x15 -> x16, waiting for transfers between devices: 5.61 us -> 19 us  [move(): return lax.ppermute(value, AXES, pairs)]
    unnamed x16 -> x0, local copies, waits for them, and re-layouts: 4.23 us -> none
    all_to_all x1, blocking collectives: 18.6 us -> 15 us  [per_device(): sums = lax.all_to_all(parts, AXES, 0, 0, tiled=True)]
    pallas_call x24 -> x18, Pallas kernels: 6.94 us -> 9.22 us  [local_call(): pl.pallas_call(body, out_shape=[jax.ShapeDtypeStruct(s, F32) for s in out...]
  transfers between devices with their start and end apart: 15 -> 16, of which waited for: 7 -> 8; matrix products, arithmetic and copies ran while one was open for 0% -> 0% of each run, Pallas kernels for 2% -> 3%
where the time goes in v3:
time: 62.3 us; the launch traced here: 62.2 us
  waiting for transfers between devices  19 us (30%)
  starting transfers between devices  18.2 us (29%)
  blocking collectives  15 us (24%)
  Pallas kernels  9.22 us (15%)
  between operations  0.74 us (1%)
    ppermute x16, waiting for transfers between devices, move(): return lax.ppermute(value, AXES, pairs)  19 us
    ppermute x16, starting transfers between devices, move(): return lax.ppermute(value, AXES, pairs)  18.2 us
    all_to_all x1, blocking collectives, per_device(): sums = lax.all_to_all(parts, AXES, 0, 0, tiled=True)  15 us
    pallas_call x18, Pallas kernels, local_call(): pl.pallas_call(body, out_shape=[jax.ShapeDtypeStruct(s, F32) for s in out...  9.22 us
  transfers between devices with their start and end apart: 16, of which 8 were waited for; matrix products, arithmetic and copies ran while one was open for 0% of the time, Pallas kernels for 3%

profile of v3, /device:TPU:0, one launch (start us, length us, event | category | flops | bytes accessed | tf_op | source)
XLA Modules:
  0.0 62.2 jit_solution(8985241688658029772)
XLA Ops:
  0.6 1.3 %shard_map.103 = (f32[256,256]{1,0:T(8,128)S(1)}, f32[4,256]{1,0:T(4,128)S(1)}) custom-call(f32[1,256]{1,0:T(1,128)} %bitcast.12, f32[1,256]{1,0:T(1,128)} %bitcast.13, s32[2,2]{1,0:T(2,128)} %pattern_h.1, f32[256,256]{1,0:T(8,128)} %coup_h.1), custom_call_target="tpu_custom_call" | custom-call | flops 200000 | bytes 1000 | tf_op jit(solution)/shard_map/pallas_call | solution.py:20
  1.9 1.5 %shard_map.105 = (f32[640,256]{1,0:T(8,128)S(1)}, f32[256,256]{1,0:T(8,128)S(1)}) custom-call(f32[256,256]{1,0:T(8,128)} %raw_h.1, f32[256,256]{1,0:T(8,128)} %craw_h.1, f32[1,256]{1,0:T(1,128)} %bitcast.14, f32[256,128]{1,0:T(8,128)} %pro_h.1, f32[4,256]{1,0:T(4,128)S(1)} %get-tuple-element.45.sent, f32[256,256]{1,0:T(8,128)S(1)} %get-tuple-element.50.cm), custom_call_target="tpu_custom_call" | custom-call | flops 100000000 | bytes 1000 | tf_op jit(solution)/shard_map/pallas_call | solution.py:20
  3.4 0.6 collective-permute-start.3
  4.1 10.6 %collective-permute-done.6.up = f32[256,256]{1,0:T(8,128)S(1)} collective-permute-done((f32[256,256]{1,0:T(8,128)S(1)}, f32[256,256]{1,0:T(8,128)S(1)}, u32[]{:S(2)}, u32[]{:S(2)}) %collective-permute-start.6) | collective-permute-done | bytes 262176 | tf_op jit(solution)/shard_map/ppermute | solution.py:408
  14.6 0.5 collective-permute-start
  15.1 1.0 %collective-permute-done.inner = f32[4,256]{1,0:T(4,128)S(1)} collective-permute-done((f32[4,256]{1,0:T(4,128)S(1)}, f32[4,256]{1,0:T(4,128)S(1)}, u32[]{:S(2)}, u32[]{:S(2)}) %collective-permute-start) | collective-permute-done | bytes 4128 | tf_op jit(solution)/shard_map/ppermute | solution.py:408
  16.7 2.5 %collective-permute-done.1.goteven = f32[2,256]{1,0:T(2,128)S(1)} collective-permute-done((f32[2,256]{1,0:T(2,128)S(1)}, f32[2,256]{1,0:T(2,128)S(1)}, u32[]{:S(2)}, u32[]{:S(2)}) %collective-permute-start.1) | collective-permute-done | bytes 2080 | tf_op jit(solution)/shard_map/ppermute | solution.py:408
  19.3 0.5 shard_map.107
  19.7 2.7 %collective-permute-start.4 = (f32[2,256]{1,0:T(2,128)S(1)}, f32[2,256]{1,0:T(2,128)S(1)}, u32[]{:S(2)}, u32[]{:S(2)}) collective-permute-start(f32[2,256]{1,0:T(2,128)S(1)} %get-tuple-element.62), channel_id=1, source_target_pairs={{1,2},{5,6},{9,10},{13,14},{17,18},{21,22},{25,26},{29,30},{0,3},{... | collective-permute-start | bytes 6152 | tf_op jit(solution)/shard_map/ppermute | solution.py:408
  22.9 0.9 %collective-permute-done.4.goteven = f32[2,256]{1,0:T(2,128)S(1)} collective-permute-done((f32[2,256]{1,0:T(2,128)S(1)}, f32[2,256]{1,0:T(2,128)S(1)}, u32[]{:S(2)}, u32[]{:S(2)}) %collective-permute-start.4) | collective-permute-done | bytes 2080 | tf_op jit(solution)/shard_map/ppermute | solution.py:408
  24.1 2.7 %collective-permute-start.8 = (f32[1,256]{1,0:T(1,128)S(1)}, f32[1,256]{1,0:T(1,128)S(1)}, u32[]{:S(2)}, u32[]{:S(2)}) collective-permute-start(f32[1,256]{1,0:T(1,128)S(1)} %get-tuple-element.70), channel_id=1, source_target_pairs={{1,2},{5,6},{9,10},{13,14},{17,18},{21,22},{25,26},{29,30},{0,3},{... | collective-permute-start | bytes 3080 | tf_op jit(solution)/shard_map/ppermute | solution.py:408
  27.1 1.0 %collective-permute-done.8.goteven = f32[1,256]{1,0:T(1,128)S(1)} collective-permute-done((f32[1,256]{1,0:T(1,128)S(1)}, f32[1,256]{1,0:T(1,128)S(1)}, u32[]{:S(2)}, u32[]{:S(2)}) %collective-permute-start.8) | collective-permute-done | bytes 1056 | tf_op jit(solution)/shard_map/ppermute | solution.py:408
  28.2 0.4 shard_map.112
  28.6 2.7 %collective-permute-start.10 = (f32[2,256]{1,0:T(2,128)S(1)}, f32[2,256]{1,0:T(2,128)S(1)}, u32[]{:S(2)}, u32[]{:S(2)}) collective-permute-start(f32[2,256]{1,0:T(2,128)S(1)} %get-tuple-element.73), channel_id=1, source_target_pairs={{1,2},{5,6},{9,10},{13,14},{17,18},{21,22},{25,26},{29,30},{0,3},{... | collective-permute-start | bytes 6152 | tf_op jit(solution)/shard_map/ppermute | solution.py:408
  31.6 1.0 %collective-permute-done.10.goteven = f32[2,256]{1,0:T(2,128)S(1)} collective-permute-done((f32[2,256]{1,0:T(2,128)S(1)}, f32[2,256]{1,0:T(2,128)S(1)}, u32[]{:S(2)}, u32[]{:S(2)}) %collective-permute-start.10) | collective-permute-done | bytes 2080 | tf_op jit(solution)/shard_map/ppermute | solution.py:408
  33.0 3.5 %collective-permute-start.12 = (f32[1,256]{1,0:T(1,128)S(1)}, f32[1,256]{1,0:T(1,128)S(1)}, u32[]{:S(2)}, u32[]{:S(2)}) collective-permute-start(f32[1,256]{1,0:T(1,128)S(1)} %get-tuple-element.77), channel_id=1, source_target_pairs={{1,2},{5,6},{9,10},{13,14},{17,18},{21,22},{25,26},{29,30},{0,3},{... | collective-permute-start | bytes 3080 | tf_op jit(solution)/shard_map/ppermute | solution.py:408
  36.8 1.0 %collective-permute-done.12.goteven = f32[1,256]{1,0:T(1,128)S(1)} collective-permute-done((f32[1,256]{1,0:T(1,128)S(1)}, f32[1,256]{1,0:T(1,128)S(1)}, u32[]{:S(2)}, u32[]{:S(2)}) %collective-permute-start.12) | collective-permute-done | bytes 1056 | tf_op jit(solution)/shard_map/ppermute | solution.py:408
  37.9 0.4 shard_map.116
  38.3 4.3 %collective-permute-start.14 = (f32[2,256]{1,0:T(2,128)S(1)}, f32[2,256]{1,0:T(2,128)S(1)}, u32[]{:S(2)}, u32[]{:S(2)}) collective-permute-start(f32[2,256]{1,0:T(2,128)S(1)} %get-tuple-element.80), channel_id=1, source_target_pairs={{1,2},{5,6},{9,10},{13,14},{17,18},{21,22},{25,26},{29,30},{0,3},{... | collective-permute-start | bytes 6152 | tf_op jit(solution)/shard_map/ppermute | solution.py:408
  42.9 1.0 %collective-permute-done.14.goteven = f32[2,256]{1,0:T(2,128)S(1)} collective-permute-done((f32[2,256]{1,0:T(2,128)S(1)}, f32[2,256]{1,0:T(2,128)S(1)}, u32[]{:S(2)}, u32[]{:S(2)}) %collective-permute-start.14) | collective-permute-done | bytes 2080 | tf_op jit(solution)/shard_map/ppermute | solution.py:408
  43.9 0.9 %shard_map.118 = (f32[4,256]{1,0:T(4,128)}, f32[1,256]{1,0:T(1,128)}, f32[1,256]{1,0:T(1,128)}, f32[2,256]{1,0:T(2,128)S(1)}) custom-call(f32[2,256]{1,0:T(2,128)S(1)} %collective-permute-done.14.goteven, f32[2,256]{1,0:T(2,128)S(1)} %collective-permute-done.15.gotodd, f32[4,256]{1,0:T(4,128)S(1)} %get-tuple-element.82.half, f32[2,256]{1,0:T(2,128)S(1)} %shard_map.117.owed, ...), custom_call_target="tpu_custom_call" | custom-call | flops 200000 | bytes 1000 | tf_op jit(solution)/shard_map/pallas_call | solution.py:20
  44.9 0.7 %shard_map.119 = f32[32,128]{1,0:T(8,128)S(1)} custom-call(f32[4,256]{1,0:T(4,128)S(1)} %get-tuple-element.45.sent, f32[2,256]{1,0:T(2,128)S(1)} %get-tuple-element.69.own0, f32[2,256]{1,0:T(2,128)S(1)} %get-tuple-element.76.own1, f32[2,256]{1,0:T(2,128)S(1)} %get-tuple-element.83.own2), custom_call_target="tpu_custom_call" | custom-call | flops 200000 | bytes 1000 | tf_op jit(solution)/shard_map/pallas_call | solution.py:20
  45.5 15.0 %all_to_all.11 = f32[32,1,128]{2,1,0:T(1,128)S(1)} all-to-all(f32[32,1,128]{2,1,0:T(1,128)S(1)} %bitcast.11), channel_id=1, replica_groups=mesh['dom'=16,'sub'=2] {'dom','sub'}, dimensions={0} | all-to-all | bytes 32768 | tf_op jit(solution)/shard_map/all_to_all | solution.py:494
  60.6 1.6 %shard_map.120 = (f32[1,256]{1,0:T(1,128)}, f32[1,256]{1,0:T(1,128)}, f32[1,3]{1,0:T(1,128)}) custom-call(f32[32,128]{1,0:T(8,128)S(1)} %bitcast.10, f32[4,256]{1,0:T(4,128)S(1)} %get-tuple-element.45.sent, f32[2,256]{1,0:T(2,128)S(1)} %get-tuple-element.69.own0, f32[2,256]{1,0:T(2,128)S(1)} %get-tuple-element.76.own1, f32[2,256]{1,0:T(2,128)S(1)} %get-tuple-element.83.own2), custom_call_target="tpu_custom_call" | custom-call | flops 200000 | bytes 1000 | tf_op jit(solution)/shard_map/pallas_call | solution.py:20
  (27 shorter events, 2.9 us)
Async XLA Ops:
  3.4 13.0 %collective-permute-start.3 = (f32[640,256]{1,0:T(8,128)S(1)}, f32[640,256]{1,0:T(8,128)S(1)}, u32[]{:S(2)}, u32[]{:S(2)}) collective-permute-start(f32[640,256]{1,0:T(8,128)S(1)} %get-tuple-element.52.packed), channel_id=1, source_target_pairs={{0,1},{1,0},{2,3},{3,2},{4,5},{5,4},{6,7},{7,6},{8,9},{9,8},{10,11... | collective-permute-start | bytes 1966088 | tf_op jit(solution)/shard_map/ppermute | solution.py:408
  4.0 10.6 %collective-permute-start.6 = (f32[256,256]{1,0:T(8,128)S(1)}, f32[256,256]{1,0:T(8,128)S(1)}, u32[]{:S(2)}, u32[]{:S(2)}) collective-permute-start(f32[256,256]{1,0:T(8,128)S(1)} %get-tuple-element.50.cm), channel_id=1, source_target_pairs={{0,1},{1,2},{2,3},{3,4},{4,5},{5,6},{6,7},{7,8},{8,9},{9,10},{10,1... | collective-permute-start | bytes 786440 | tf_op jit(solution)/shard_map/ppermute | solution.py:408
  14.6 8.0 %collective-permute-start.7 = (f32[256,256]{1,0:T(8,128)S(1)}, f32[256,256]{1,0:T(8,128)S(1)}, u32[]{:S(2)}, u32[]{:S(2)}) collective-permute-start(f32[256,256]{1,0:T(8,128)S(1)} %collective-permute-done.6.up), channel_id=1, source_target_pairs={{0,1},{1,0},{2,3},{3,2},{4,5},{5,4},{6,7},{7,6},{8,9},{9,8},{10,11... | collective-permute-start | bytes 786440 | tf_op jit(solution)/shard_map/ppermute | solution.py:408
  14.6 1.5 %collective-permute-start = (f32[4,256]{1,0:T(4,128)S(1)}, f32[4,256]{1,0:T(4,128)S(1)}, u32[]{:S(2)}, u32[]{:S(2)}) collective-permute-start(f32[4,256]{1,0:T(4,128)S(1)} %get-tuple-element.45.sent), channel_id=1, source_target_pairs={{0,1},{1,0},{2,3},{3,2},{4,5},{5,4},{6,7},{7,6},{8,9},{9,8},{10,11... | collective-permute-start | bytes 12296 | tf_op jit(solution)/shard_map/ppermute | solution.py:408
  16.2 3.1 %collective-permute-start.1 = (f32[2,256]{1,0:T(2,128)S(1)}, f32[2,256]{1,0:T(2,128)S(1)}, u32[]{:S(2)}, u32[]{:S(2)}) collective-permute-start(f32[2,256]{1,0:T(2,128)S(1)} %get-tuple-element.46), channel_id=1, source_target_pairs={{1,2},{5,6},{9,10},{13,14},{17,18},{21,22},{25,26},{29,30},{0,3},{... | collective-permute-start | bytes 6152 | tf_op jit(solution)/shard_map/ppermute | solution.py:408
  16.3 3.0 %collective-permute-start.2 = (f32[2,256]{1,0:T(2,128)S(1)}, f32[2,256]{1,0:T(2,128)S(1)}, u32[]{:S(2)}, u32[]{:S(2)}) collective-permute-start(f32[2,256]{1,0:T(2,128)S(1)} %get-tuple-element.47), channel_id=1, source_target_pairs={{3,4},{7,8},{11,12},{15,16},{19,20},{23,24},{27,28},{0,1},{2,5},{6... | collective-permute-start | bytes 6152 | tf_op jit(solution)/shard_map/ppermute | solution.py:408
  19.7 4.0 %collective-permute-start.4 = (f32[2,256]{1,0:T(2,128)S(1)}, f32[2,256]{1,0:T(2,128)S(1)}, u32[]{:S(2)}, u32[]{:S(2)}) collective-permute-start(f32[2,256]{1,0:T(2,128)S(1)} %get-tuple-element.62), channel_id=1, source_target_pairs={{1,2},{5,6},{9,10},{13,14},{17,18},{21,22},{25,26},{29,30},{0,3},{... | collective-permute-start | bytes 6152 | tf_op jit(solution)/shard_map/ppermute | solution.py:408
  22.5 1.3 %collective-permute-start.5 = (f32[2,256]{1,0:T(2,128)S(1)}, f32[2,256]{1,0:T(2,128)S(1)}, u32[]{:S(2)}, u32[]{:S(2)}) collective-permute-start(f32[2,256]{1,0:T(2,128)S(1)} %get-tuple-element.63), channel_id=1, source_target_pairs={{3,4},{7,8},{11,12},{15,16},{19,20},{23,24},{27,28},{0,1},{2,5},{6... | collective-permute-start | bytes 6152 | tf_op jit(solution)/shard_map/ppermute | solution.py:408
  24.1 4.0 %collective-permute-start.8 = (f32[1,256]{1,0:T(1,128)S(1)}, f32[1,256]{1,0:T(1,128)S(1)}, u32[]{:S(2)}, u32[]{:S(2)}) collective-permute-start(f32[1,256]{1,0:T(1,128)S(1)} %get-tuple-element.70), channel_id=1, source_target_pairs={{1,2},{5,6},{9,10},{13,14},{17,18},{21,22},{25,26},{29,30},{0,3},{... | collective-permute-start | bytes 3080 | tf_op jit(solution)/shard_map/ppermute | solution.py:408
  26.8 1.3 %collective-permute-start.9 = (f32[1,256]{1,0:T(1,128)S(1)}, f32[1,256]{1,0:T(1,128)S(1)}, u32[]{:S(2)}, u32[]{:S(2)}) collective-permute-start(f32[1,256]{1,0:T(1,128)S(1)} %get-tuple-element.71), channel_id=1, source_target_pairs={{3,4},{7,8},{11,12},{15,16},{19,20},{23,24},{27,28},{0,1},{2,5},{6... | collective-permute-start | bytes 3080 | tf_op jit(solution)/shard_map/ppermute | solution.py:408
  28.6 4.0 %collective-permute-start.10 = (f32[2,256]{1,0:T(2,128)S(1)}, f32[2,256]{1,0:T(2,128)S(1)}, u32[]{:S(2)}, u32[]{:S(2)}) collective-permute-start(f32[2,256]{1,0:T(2,128)S(1)} %get-tuple-element.73), channel_id=1, source_target_pairs={{1,2},{5,6},{9,10},{13,14},{17,18},{21,22},{25,26},{29,30},{0,3},{... | collective-permute-start | bytes 6152 | tf_op jit(solution)/shard_map/ppermute | solution.py:408
  31.3 1.3 %collective-permute-start.11 = (f32[2,256]{1,0:T(2,128)S(1)}, f32[2,256]{1,0:T(2,128)S(1)}, u32[]{:S(2)}, u32[]{:S(2)}) collective-permute-start(f32[2,256]{1,0:T(2,128)S(1)} %get-tuple-element.74), channel_id=1, source_target_pairs={{3,4},{7,8},{11,12},{15,16},{19,20},{23,24},{27,28},{0,1},{2,5},{6... | collective-permute-start | bytes 6152 | tf_op jit(solution)/shard_map/ppermute | solution.py:408
  33.0 4.8 %collective-permute-start.12 = (f32[1,256]{1,0:T(1,128)S(1)}, f32[1,256]{1,0:T(1,128)S(1)}, u32[]{:S(2)}, u32[]{:S(2)}) collective-permute-start(f32[1,256]{1,0:T(1,128)S(1)} %get-tuple-element.77), channel_id=1, source_target_pairs={{1,2},{5,6},{9,10},{13,14},{17,18},{21,22},{25,26},{29,30},{0,3},{... | collective-permute-start | bytes 3080 | tf_op jit(solution)/shard_map/ppermute | solution.py:408
  36.5 1.3 %collective-permute-start.13 = (f32[1,256]{1,0:T(1,128)S(1)}, f32[1,256]{1,0:T(1,128)S(1)}, u32[]{:S(2)}, u32[]{:S(2)}) collective-permute-start(f32[1,256]{1,0:T(1,128)S(1)} %get-tuple-element.78), channel_id=1, source_target_pairs={{3,4},{7,8},{11,12},{15,16},{19,20},{23,24},{27,28},{0,1},{2,5},{6... | collective-permute-start | bytes 3080 | tf_op jit(solution)/shard_map/ppermute | solution.py:408
  38.3 5.6 %collective-permute-start.14 = (f32[2,256]{1,0:T(2,128)S(1)}, f32[2,256]{1,0:T(2,128)S(1)}, u32[]{:S(2)}, u32[]{:S(2)}) collective-permute-start(f32[2,256]{1,0:T(2,128)S(1)} %get-tuple-element.80), channel_id=1, source_target_pairs={{1,2},{5,6},{9,10},{13,14},{17,18},{21,22},{25,26},{29,30},{0,3},{... | collective-permute-start | bytes 6152 | tf_op jit(solution)/shard_map/ppermute | solution.py:408
  42.6 1.3 %collective-permute-start.15 = (f32[2,256]{1,0:T(2,128)S(1)}, f32[2,256]{1,0:T(2,128)S(1)}, u32[]{:S(2)}, u32[]{:S(2)}) collective-permute-start(f32[2,256]{1,0:T(2,128)S(1)} %get-tuple-element.81), channel_id=1, source_target_pairs={{3,4},{7,8},{11,12},{15,16},{19,20},{23,24},{27,28},{0,1},{2,5},{6... | collective-permute-start | bytes 6152 | tf_op jit(solution)/shard_map/ppermute | solution.py:408
